TPU v7x, 256 devices: a whole 4x4x8 slice. The times are simulated.
256 devices in a mesh: gx: 4 (over x), gy: 64 (over z, y, core).
Axes of the slice: x: 4, y: 4, z: 8, core: 2. Of those that a mesh axis runs over, the one named last changes fastest.
Arguments:
- features: bfloat16 [262144, 768], P(('gx', 'gy')), may hold values from -6 to 6
- seed_rows: int32 [16384], P(('gx', 'gy')), may hold values from 0 to 1023
- hop1_ids: int32 [16384, 5], P(('gx', 'gy')), may hold values from 0 to 262143, as said below
- hop2_ids: int32 [16384, 5, 5], P(('gx', 'gy')), may hold values from 0 to 262143, as said below
- w_self: bfloat16 [768, 1024], replicated, may hold values from -0.21875 to 0.21875
- w_neigh: bfloat16 [768, 1024], replicated, may hold values from -0.21875 to 0.21875
- bias: float32 [1024], replicated, may hold values from -3 to 3
- cotangent: bfloat16 [16384, 1024], P(('gx', 'gy')), may hold values from -6 to 6
Outputs:
- embedded: bfloat16 [16384, 1024], P(('gx', 'gy'))
- grad_self: float32 [768, 1024], P(None, ('gx', 'gy'))
- grad_neigh: float32 [768, 1024], P(None, ('gx', 'gy'))
- grad_bias: float32 [1024], P(('gx', 'gy'))
Inputs may be any that keep to these rules, and one draw needn't show every extreme that they name: `hop1_ids`: row i belongs to device i // 1024 (device index gx * 64 + gy). The 320 entries of one device name at most 2 rows of any one owner, repeats counted; in every draw one owner receives exactly 2 from every device. `hop2_ids`: row i belongs to device i // 1024. The 1600 entries of one device name at most 9 rows of any one owner, repeats counted; in every draw one owner receives exactly 9 from every device.
All inputs are finite; a program needn't handle non-finite values.
Results may differ from a plain program's by a relative error of at most 0.025.
The roundings to bfloat16 on the way count: a program that leaves them out, or rounds other values in their place, can miss the bound.
Values may be sent and summed in bfloat16 or wider, within the bound.
No kernel may reach another device: no remote copies, remote signals or barrier semaphores. Data moves between devices by JAX's collectives and lax.ppermute only.
A program may use at most 64 MiB of HBM per device.

v0:
```python
import functools

import jax
import jax.numpy as jnp
import numpy as np
from jax import lax
from jax.experimental import pallas as pl
from jax.experimental.pallas import tpu as pltpu
from jax.sharding import Mesh
from jax.sharding import PartitionSpec as P

GX_GY = ("gx", "gy_0", "gy_1", "gy_2")
FAR_CAP = 9
NEAR_CAP = 2
SLOTS = 16
MAIN = 8
EXTRA = 4
PLAN_BLOCK = 256
BF16 = jnp.bfloat16
F32 = jnp.float32
INTERPRET = False

NN = (((1,), (0,)), ((), ()))
NT = (((1,), (1,)), ((), ()))


def dot(left, right, dims=NN):
    return lax.dot_general(left, right, dims, preferred_element_type=F32)


def round_up(value, step):
    return -(-value // step) * step


def plan_kernel(devices, row_bits, far_blocks, ids_ref, base_ref, group_ref, request_ref, groups_ref):
    lanes = ids_ref.shape[1]
    block = PLAN_BLOCK
    upper = (
        lax.broadcasted_iota(jnp.int32, (block, block), 0) < lax.broadcasted_iota(jnp.int32, (block, block), 1)
    ).astype(F32).astype(BF16)
    owner_at = lax.broadcasted_iota(jnp.int32, (devices, block), 0)
    slot_at = lax.broadcasted_iota(jnp.int32, (SLOTS, block), 0)
    carry = jnp.zeros((devices, 1), F32)
    request = jnp.zeros((devices, SLOTS), F32)
    groups = jnp.zeros((devices, SLOTS), F32)
    for at in range(lanes // block):
        here = slice(at * block, (at + 1) * block)
        ids = ids_ref[:, here]
        if at == far_blocks:
            carry = jnp.zeros((devices, 1), F32)
        match = (owner_at == lax.shift_right_arithmetic(ids, row_bits)).astype(F32)
        match_low = match.astype(BF16)
        before = dot(match_low, upper) + carry
        carry = carry + jnp.sum(match, axis=1, keepdims=True)
        rank = jnp.sum(match * before, axis=0, keepdims=True)
        slot = rank.astype(jnp.int32) + base_ref[:, here]
        placed = (slot_at == slot).astype(F32)
        local = ids & ((1 << row_bits) - 1)
        low = local & 31
        group = group_ref[:, here]
        group_low = group & 31
        request = request + dot(match_low, (placed * (local - low).astype(F32)).astype(BF16), NT)
        request = request + dot(match_low, (placed * low.astype(F32)).astype(BF16), NT)
        groups = groups + dot(match_low, (placed * (group - group_low).astype(F32)).astype(BF16), NT)
        groups = groups + dot(match_low, (placed * group_low.astype(F32)).astype(BF16), NT)
    request_ref[...] = request.astype(jnp.int32)
    groups_ref[...] = groups.astype(jnp.int32) - 1


def plan(near_ids, far_ids, devices, row_bits):
    seeds, fan_one = near_ids.shape
    fan_two = far_ids.shape[2]
    far_total = seeds * fan_one * fan_two
    near_total = seeds * fan_one
    far_lanes = round_up(far_total, PLAN_BLOCK)
    near_lanes = round_up(near_total, PLAN_BLOCK)
    ids = jnp.concatenate(
        [
            jnp.pad(far_ids.reshape(1, -1), ((0, 0), (0, far_lanes - far_total)), constant_values=-1),
            jnp.pad(near_ids.reshape(1, -1), ((0, 0), (0, near_lanes - near_total)), constant_values=-1),
        ],
        axis=1,
    )
    lanes = far_lanes + near_lanes
    base = np.zeros((1, lanes), np.int32)
    base[:, far_lanes:] = FAR_CAP
    group = np.zeros((1, lanes), np.int32)
    far_at = np.arange(far_total)
    group[0, :far_total] = (far_at // fan_two) % fan_one * seeds + far_at // (fan_one * fan_two) + 1
    near_at = np.arange(near_total)
    group[0, far_lanes : far_lanes + near_total] = near_at % fan_one * seeds + near_at // fan_one + 1
    out = jax.ShapeDtypeStruct((devices, SLOTS), jnp.int32)
    return pl.pallas_call(
        lambda *refs: plan_kernel(devices, row_bits, far_lanes // PLAN_BLOCK, *refs),
        out_shape=(out, out),
        name="plan",
        interpret=INTERPRET,
    )(ids, jnp.asarray(base), jnp.asarray(group))


def serve_kernel(asked_ref, features_ref, out_ref):
    peers = asked_ref.shape[0]
    rows_dev, width = features_ref.shape
    half = width // 2
    asked = jnp.broadcast_to(asked_ref[...].astype(F32), (peers, MAIN, SLOTS))
    lane = lax.broadcasted_iota(jnp.int32, (peers, MAIN, SLOTS), 2)
    place = lax.broadcasted_iota(jnp.int32, (peers, MAIN, SLOTS), 1)
    row_at = lax.broadcasted_iota(jnp.int32, (peers, MAIN, rows_dev), 2).astype(F32)

    def rows_of(slot):
        chosen = jnp.sum(jnp.where(lane == slot, asked, 0.0), axis=2, keepdims=True)
        picks = (row_at == chosen).astype(F32).reshape(peers * MAIN, rows_dev).astype(BF16)
        return dot(picks, features_ref[...])

    out_ref[:, :width] = rows_of(place).astype(BF16)
    extra = rows_of(MAIN + place % EXTRA)
    part = lax.broadcasted_iota(jnp.int32, (peers * MAIN, half), 0) % MAIN
    out_ref[:, width:] = jnp.where(part < EXTRA, extra[:, :half], extra[:, half:]).astype(BF16)


def serve(asked, features, steps=8):
    devices = asked.shape[0]
    rows_dev, width = features.shape
    peers = devices // steps
    payload = width + width // 2
    return pl.pallas_call(
        serve_kernel,
        grid=(steps,),
        in_specs=[
            pl.BlockSpec((peers, 1, SLOTS), lambda i: (i, 0, 0)),
            pl.BlockSpec((rows_dev, width), lambda i: (0, 0)),
        ],
        out_specs=pl.BlockSpec((peers * MAIN, payload), lambda i: (i, 0)),
        out_shape=jax.ShapeDtypeStruct((devices * MAIN, payload), BF16),
        name="serve",
        interpret=INTERPRET,
    )(asked, features)


def layer_kernel(
    take_steps, fan_one, fan_two, rows_ref, main_ref, far_ref, near_ref, seed_ref, self_ref, neigh_ref,
    bias_ref, spread_ref, embedded_ref, grad_ref, far_acc, near_acc, own, pooled,
):
    step = pl.program_id(0)
    seeds, width = seed_ref.shape
    half = width // 2
    near_total = near_acc.shape[0]

    @pl.when(step == 0)
    def _():
        far_acc[...] = jnp.zeros_like(far_acc)
        near_acc[...] = jnp.zeros_like(near_acc)

    @pl.when(step < take_steps)
    def _():
        lanes = rows_ref.shape[0]
        group_at = lax.broadcasted_iota(jnp.int32, (near_total, lanes), 0)
        first = lax.broadcasted_iota(jnp.int32, (1, lanes), 1) % MAIN < EXTRA

        def picks(groups):
            return (group_at == groups).astype(F32).astype(BF16)

        extra = rows_ref[:, width:]
        far = far_ref[...]
        near = near_ref[...]
        far_acc[...] += dot(picks(main_ref[...]), rows_ref[:, :width])
        far_acc[:, :half] += dot(picks(jnp.where(first, far, -1)), extra)
        far_acc[:, half:] += dot(picks(jnp.where(first, -1, far)), extra)
        near_acc[:, :half] += dot(picks(jnp.where(first, near, -1)), extra)
        near_acc[:, half:] += dot(picks(jnp.where(first, -1, near)), extra)

    @pl.when(step == take_steps - 1)
    def _():
        own[:near_total] = near_acc[...].astype(BF16)
        own[near_total:] = seed_ref[...]
        pooled[:near_total] = (far_acc[...] / fan_two).astype(BF16)
        summed = near_acc[:seeds]
        for k in range(1, fan_one):
            summed = summed + near_acc[k * seeds : (k + 1) * seeds]
        pooled[near_total:] = (summed / fan_one).astype(BF16)

    @pl.when(step >= take_steps)
    def _():
        pre = dot(own[...], self_ref[...]) + dot(pooled[...], neigh_ref[...]) + bias_ref[...]
        hidden = jnp.maximum(pre, 0.0).astype(BF16).astype(F32)
        summed = hidden[near_total:]
        for k in range(fan_one):
            summed = summed + hidden[k * seeds : (k + 1) * seeds]
        embedded_ref[...] = (summed / (1 + fan_one)).astype(BF16)
        spread = spread_ref[...].astype(F32)
        delta = jnp.where(pre > 0, jnp.concatenate([spread] * (1 + fan_one), axis=0), 0.0)
        turned = delta.T.astype(BF16)
        grad_ref[:, :width] = dot(turned, own[...]).astype(BF16)
        grad_ref[:, width : 2 * width] = dot(turned, pooled[...]).astype(BF16)
        ones = (lax.broadcasted_iota(jnp.int32, (delta.shape[0], 128), 1) == 0).astype(F32).astype(BF16)
        grad_ref[:, 2 * width :] = dot(turned, ones).astype(BF16)


def layer(rows, main, far, near, seed_x, w_self, w_neigh, bias, spread, fan_one, fan_two, take_steps=8, hidden_steps=4):
    total, payload = rows.shape
    seeds, width = seed_x.shape
    hidden = w_self.shape[1]
    lanes = total // take_steps
    part = hidden // hidden_steps
    near_total = seeds * fan_one
    steps = take_steps + hidden_steps
    early = lambda i: jnp.minimum(i, take_steps - 1)
    late = lambda i: jnp.maximum(i - take_steps, 0)
    groups = pl.BlockSpec((1, lanes), lambda i: (0, early(i)))
    weights = pl.BlockSpec((width, part), lambda i: (0, late(i)))
    return pl.pallas_call(
        functools.partial(layer_kernel, take_steps, fan_one, fan_two),
        grid=(steps,),
        in_specs=[
            pl.BlockSpec((lanes, payload), lambda i: (early(i), 0)),
            groups,
            groups,
            groups,
            pl.BlockSpec((seeds, width), lambda i: (0, 0)),
            weights,
            weights,
            pl.BlockSpec((1, part), lambda i: (0, late(i))),
            pl.BlockSpec((seeds, part), lambda i: (0, late(i))),
        ],
        out_specs=(
            pl.BlockSpec((seeds, part), lambda i: (0, late(i))),
            pl.BlockSpec((part, 2 * width + 128), lambda i: (late(i), 0)),
        ),
        out_shape=(
            jax.ShapeDtypeStruct((seeds, hidden), BF16),
            jax.ShapeDtypeStruct((hidden, 2 * width + 128), BF16),
        ),
        scratch_shapes=[
            pltpu.VMEM((near_total, width), F32),
            pltpu.VMEM((near_total, width), F32),
            pltpu.VMEM((near_total + seeds, width), BF16),
            pltpu.VMEM((near_total + seeds, width), BF16),
        ],
        name="layer",
        interpret=INTERPRET,
    )(rows, main, far, near, seed_x, w_self, w_neigh, bias, spread)


def exchange(pieces, axes):
    return lax.all_to_all(pieces, axes, split_axis=0, concat_axis=0, tiled=True)


def slot_lanes(groups, devices):
    main = groups[:, :MAIN].reshape(1, -1)
    extra = groups[:, MAIN : MAIN + EXTRA]
    at = jnp.arange(EXTRA, dtype=jnp.int32)[None, :]
    far = jnp.where(at < FAR_CAP - MAIN, extra, -1)
    near = jnp.where(at >= FAR_CAP - MAIN, extra, -1)
    twice = lambda x: jnp.concatenate([x, x], axis=1).reshape(1, -1)
    return main, twice(far), twice(near)


def body(features, seed_rows, hop1_ids, hop2_ids, w_self, w_neigh, bias, cotangent):
    sizes = [lax.axis_size(a) for a in GX_GY]
    split_x, split_z, split_y, split_c = sizes
    devices = split_x * split_z * split_y * split_c
    rows_dev, width = features.shape
    row_bits = rows_dev.bit_length() - 1
    hidden = w_self.shape[1]
    fan_one = hop1_ids.shape[1]
    fan_two = hop2_ids.shape[2]
    share = hidden // devices

    request, groups = plan(hop1_ids, hop2_ids, devices, row_bits)
    asked = exchange(request.reshape(devices, 1, SLOTS), GX_GY)
    served = serve(asked, features)
    rows = exchange(served.reshape(devices, MAIN, -1), GX_GY).reshape(devices * MAIN, -1)

    order = np.arange(hidden, dtype=np.int32).reshape(*sizes, share)
    order = np.transpose(order, (3, 0, 2, 1, 4)).reshape(1, hidden)
    turn = (lax.broadcasted_iota(jnp.int32, (hidden, hidden), 0) == jnp.asarray(order)).astype(BF16)
    self_turned = dot(w_self, turn).astype(BF16)
    neigh_turned = dot(w_neigh, turn).astype(BF16)
    bias_turned = bias[jnp.asarray(order[0])][None, :]
    spread = (cotangent.astype(F32) / (1 + fan_one)).astype(BF16)
    spread_turned = dot(spread, turn).astype(BF16)
    seed_x = features[seed_rows]
    main, far, near = slot_lanes(groups, devices)

    embedded_turned, grad = layer(
        rows, main, far, near, seed_x, self_turned, neigh_turned, bias_turned, spread_turned, fan_one, fan_two
    )
    embedded = dot(embedded_turned, turn, NT).astype(BF16)

    for axes, count in ((("gy_2",), split_c), (("gx", "gy_1"), split_x * split_y), (("gy_0",), split_z)):
        pieces = exchange(grad.reshape(count, -1, grad.shape[-1]), axes)
        grad = pieces.astype(F32).sum(axis=0)
        if axes != ("gy_0",):
            grad = grad.astype(BF16)
    return (embedded, grad[:, :width].T, grad[:, width : 2 * width].T, grad[:, 2 * width])


def solution(mesh):
    split = Mesh(mesh.devices.reshape(mesh.shape["gx"], 8, 4, 2), GX_GY)
    rows = P(GX_GY, None)
    in_specs = (rows, P(GX_GY), rows, P(GX_GY, None, None), P(), P(), P(), rows)
    out_specs = (rows, P(None, GX_GY), P(None, GX_GY), P(GX_GY))
    return jax.shard_map(body, mesh=split, in_specs=in_specs, out_specs=out_specs, check_vma=False)
```

profile of v0, /device:TPU:8, one launch (start us, length us, event | category | flops | bytes accessed | tf_op | source)
XLA Modules:
  0.0 236.6 jit_solution(16545357694179467122)
XLA Ops:
  0.6 0.0 copy-start
  0.6 1.0 copy.44
  1.7 0.2 reshape.51
  1.9 0.8 copy.45
  2.6 0.1 reshape.52
  2.8 0.6 fusion.15.refs_0_
  3.4 4.8 %plan.1 = (s32[256,16]{1,0:T(8,128)}, s32[256,16]{1,0:T(8,128)}) custom-call(s32[1,2304]{1,0:T(1,128)} %fusion.15.refs_0_, s32[1,2304]{1,0:T(1,128)} %constant.26.clone.refs_1_, s32[1,2304]{1,0:T(1,128)} %constant.27.clone.refs_2_), custom_call_target="tpu_custom_call" | custom-call | tf_op jit(solution)/shard_map/plan/pallas_call | solution.py:93
  8.2 26.9 %all_to_all.25.asked_ref = s32[256,1,16]{2,1,0:T(1,128)} all-to-all(s32[256,1,16]{2,1,0:T(1,128)} %bitcast.22), channel_id=1, replica_groups=mesh['gx'=4,'gy_0'=8,'gy_1'=4,'gy_2'=2] {'gx','gy_0','gy_1','gy_2'}, dimensions={0} | all-to-all | bytes 32768 | tf_op jit(solution)/shard_map/all_to_all | solution.py:245
  35.0 10.7 %serve.1 = bf16[2048,1152]{1,0:T(8,128)(2,1)} custom-call(s32[256,1,16]{2,1,0:T(1,128)} %all_to_all.25.asked_ref, bf16[1024,768]{1,0:T(8,128)(2,1)} %features_ref.1), custom_call_target="tpu_custom_call" | custom-call | tf_op jit(solution)/shard_map/serve/pallas_call | solution.py:126
  45.8 0.0 copy-start.3
  45.8 0.0 copy-start.8
  45.8 0.0 copy-start.2
  45.8 8.0 %all-to-all-start.1 = ((bf16[256,8,1152]{2,1,0:T(8,128)(2,1)}), bf16[256,8,1152]{2,1,0:T(8,128)(2,1)}, u32[]{:S(2)}, u32[]{:S(2)}) async-start(bf16[256,8,1152]{2,1,0:T(8,128)(2,1)} %bitcast.18), calls=%async_computation.1 | async-start | bytes 9437184 | tf_op jit(solution)/shard_map/all_to_all | solution.py:245
  53.8 0.0 copy-start.4
  53.8 0.0 copy-start.1
  53.9 0.0 copy-done.3
  53.9 0.1 slice_select_fusion
  54.0 0.1 pad_add_fusion
  54.1 0.7 reshape.57.far_ref
  54.9 0.7 reshape.58.near_ref
  55.6 0.7 reshape.56.main_ref
  56.3 0.0 copy-done.8
  56.3 0.0 copy-done.2
  56.3 1.3 gather_fusion
  57.7 0.0 copy-done.4
  57.7 0.0 copy-done.1
  57.7 0.0 copy-start.6
  57.7 8.8 %gather_fusion.1 = f32[1024]{0:T(1024)} fusion(f32[1024]{0:T(1024)S(1)} %copy-done.1, s32[1024]{0:T(1024)S(1)} %broadcast_clamp_fusion), kind=kCustom, calls=%fused_computation.1 | custom fusion | bytes 12288 | tf_op jit(solution)/shard_map/gather | solution.py:279
  66.5 0.0 copy-done.6
  66.5 1.6 fusion.12.spread_ref
  68.0 0.0 copy-done
  68.1 3.0 %fusion.10.neigh_ref = bf16[768,1024]{1,0:T(8,128)(2,1)} fusion(bf16[768,1024]{1,0:T(8,128)(2,1)S(1)} %copy-done, s32[1024]{0:T(1024)S(1)} %copy-done.4), kind=kOutput, calls=%fused_computation.13 | convolution fusion | flops 1612447744 | bytes 3149824 | tf_op jit(solution)/shard_map/dot_general | solution.py:28
  71.1 0.0 copy-done.5
  71.1 3.0 %fusion.11.self_ref = bf16[768,1024]{1,0:T(8,128)(2,1)} fusion(bf16[768,1024]{1,0:T(8,128)(2,1)S(1)} %copy-done.5, s32[1024]{0:T(1024)S(1)} %copy-done.4), kind=kOutput, calls=%fused_computation.14 | convolution fusion | flops 1612447744 | bytes 3149824 | tf_op jit(solution)/shard_map/dot_general | solution.py:28
  74.1 88.9 %all-to-all-done.1 = bf16[256,8,1152]{2,1,0:T(8,128)(2,1)} async-done(((bf16[256,8,1152]{2,1,0:T(8,128)(2,1)}), bf16[256,8,1152]{2,1,0:T(8,128)(2,1)}, u32[]{:S(2)}, u32[]{:S(2)}) %all-to-all-start.1) | async-done | bytes 4718624 | tf_op jit(solution)/shard_map/all_to_all | solution.py:245
  163.1 16.6 %layer.1 = (bf16[64,1024]{1,0:T(8,128)(2,1)}, bf16[1024,1664]{1,0:T(8,128)(2,1)}) custom-call(bf16[2048,1152]{1,0:T(8,128)(2,1)} %bitcast.2.rows_ref, s32[1,2048]{1,0:T(1,128)} %reshape.56.main_ref, s32[1,2048]{1,0:T(1,128)} %reshape.57.far_ref, s32[1,2048]{1,0:T(1,128)} %reshape.58.near_ref, bf16[64,768]{1,0:T(8,128)(2,1)} %gather_fusion, ...), custom_call_target="tpu_custom_call" | custom-call | tf_op jit(solution)/shard_map/layer/pallas_call | solution.py:211
  179.7 10.6 %all_to_all.26 = bf16[2,512,1664]{2,1,0:T(8,128)(2,1)} all-to-all(bf16[2,512,1664]{2,1,0:T(8,128)(2,1)} %bitcast.20), channel_id=1, replica_groups=mesh['gx'=4,'gy_0'=8,'gy_1'=4,'gy_2'=2] {'gy_2'}, dimensions={0} | all-to-all | bytes 6815744 | tf_op jit(solution)/shard_map/all_to_all | solution.py:245
  190.4 4.3 %reduce_sum.33 = bf16[512,1664]{1,0:T(8,128)(2,1)} reduce(bf16[2,512,1664]{2,1,0:T(8,128)(2,1)} %all_to_all.26, bf16[]{:T(256)} %constant.24.clone.1), dimensions={0}, to_apply=%region_0.1 | reduce | flops 851968 | bytes 5111810 | tf_op jit(solution)/shard_map/reduce_sum | solution.py:292
  194.7 27.6 %all_to_all.27 = bf16[16,32,1664]{2,1,0:T(8,128)(2,1)S(1)} all-to-all(bf16[16,32,1664]{2,1,0:T(8,128)(2,1)} %bitcast.19), channel_id=1, replica_groups=mesh['gx'=4,'gy_0'=8,'gy_1'=4,'gy_2'=2] {'gx','gy_1'}, dimensions={0} | all-to-all | bytes 3407872 | tf_op jit(solution)/shard_map/all_to_all | solution.py:245
  222.3 0.2 reduce_sum.34
  222.5 0.7 reshape.61
  223.2 3.4 %all-to-all-start.4 = ((bf16[8,4,1664]{2,1,0:T(4,128)(2,1)}), bf16[8,4,1664]{2,1,0:T(4,128)(2,1)S(1)}, u32[]{:S(2)}, u32[]{:S(2)}) async-start(bf16[8,4,1664]{2,1,0:T(4,128)(2,1)} %reshape.61), calls=%async_computation.4 | async-start | bytes 212992 | tf_op jit(solution)/shard_map/all_to_all | solution.py:245
  226.6 0.0 copy-done.7
  226.6 1.6 fusion.13
  228.2 7.1 %all-to-all-done.4 = bf16[8,4,1664]{2,1,0:T(4,128)(2,1)S(1)} async-done(((bf16[8,4,1664]{2,1,0:T(4,128)(2,1)}), bf16[8,4,1664]{2,1,0:T(4,128)(2,1)S(1)}, u32[]{:S(2)}, u32[]{:S(2)}) %all-to-all-start.4) | async-done | bytes 106528 | tf_op jit(solution)/shard_map/all_to_all | solution.py:245
  235.3 0.1 convert_reduce_fusion
  235.4 0.6 slice_bitcast_fusion
  236.0 0.6 slice_reduce_fusion
  (7 shorter events, 0.0 us)
Async XLA Ops:
  0.6 67.4 %copy-start = (bf16[768,1024]{1,0:T(8,128)(2,1)S(1)}, bf16[768,1024]{1,0:T(8,128)(2,1)}, u32[]{:S(2)}) copy-start(bf16[768,1024]{1,0:T(8,128)(2,1)} %param.17) | copy-start | bytes 4718596
  45.8 8.1 %copy-start.3 = (s32[256,16]{1,0:T(8,128)S(1)}, s32[256,16]{1,0:T(8,128)}, u32[]{:S(2)}) copy-start(s32[256,16]{1,0:T(8,128)} %get-tuple-element.9) | copy-start | bytes 49156
  45.8 10.5 %copy-start.8 = (s32[64]{0:T(128)S(1)}, s32[64]{0:T(128)}, u32[]{:S(2)}) copy-start(s32[64]{0:T(128)} %param.13) | copy-start | bytes 772
  45.8 10.5 %copy-start.2 = (bf16[1024,768]{1,0:T(8,128)(2,1)S(1)}, bf16[1024,768]{1,0:T(8,128)(2,1)}, u32[]{:S(2)}) copy-start(bf16[1024,768]{1,0:T(8,128)(2,1)} %features_ref.1) | copy-start | bytes 4718596
  45.8 117.3 %all-to-all-start.1 = ((bf16[256,8,1152]{2,1,0:T(8,128)(2,1)}), bf16[256,8,1152]{2,1,0:T(8,128)(2,1)}, u32[]{:S(2)}, u32[]{:S(2)}) async-start(bf16[256,8,1152]{2,1,0:T(8,128)(2,1)} %bitcast.18), calls=%async_computation.1 | async-start | bytes 9437184 | tf_op jit(solution)/shard_map/all_to_all | solution.py:245
  53.8 3.8 %copy-start.4 = (s32[1024]{0:T(1024)S(1)}, s32[1024]{0:T(1024)}, u32[]{:S(2)}) copy-start(s32[1024]{0:T(1024)} %constant.38) | copy-start | bytes 12292
  53.8 3.8 %copy-start.1 = (f32[1024]{0:T(1024)S(1)}, f32[1024]{0:T(1024)}, u32[]{:S(2)}) copy-start(f32[1024]{0:T(1024)} %param.18) | copy-start | bytes 12292
  57.7 8.8 %copy-start.6 = (bf16[64,1024]{1,0:T(8,128)(2,1)S(1)}, bf16[64,1024]{1,0:T(8,128)(2,1)}, u32[]{:S(2)}) copy-start(bf16[64,1024]{1,0:T(8,128)(2,1)} %param.19) | copy-start | bytes 393220
  68.1 3.0 %copy-start.5 = (bf16[768,1024]{1,0:T(8,128)(2,1)S(1)}, bf16[768,1024]{1,0:T(8,128)(2,1)}, u32[]{:S(2)}) copy-start(bf16[768,1024]{1,0:T(8,128)(2,1)} %param.16) | copy-start | bytes 4718596
  222.3 4.3 %copy-start.7 = (bf16[64,1024]{1,0:T(8,128)(2,1)S(1)}, bf16[64,1024]{1,0:T(8,128)(2,1)}, u32[]{:S(2)}) copy-start(bf16[64,1024]{1,0:T(8,128)(2,1)} %get-tuple-element.10) | copy-start | bytes 393220
  223.2 12.1 %all-to-all-start.4 = ((bf16[8,4,1664]{2,1,0:T(4,128)(2,1)}), bf16[8,4,1664]{2,1,0:T(4,128)(2,1)S(1)}, u32[]{:S(2)}, u32[]{:S(2)}) async-start(bf16[8,4,1664]{2,1,0:T(4,128)(2,1)} %reshape.61), calls=%async_computation.4 | async-start | bytes 212992 | tf_op jit(solution)/shard_map/all_to_all | solution.py:245
where the time goes:
time: 237 us
  waiting for transfers between devices  96.1 us (41%)
  blocking collectives  65.1 us (27%)
  Pallas kernels  32.2 us (14%)
  local copies, waits for them, and re-layouts  16.4 us (7%)
  starting transfers between devices  11.4 us (5%)
  matrix products  9.2 us (4%)
  other arithmetic  5.49 us (2%)
    all_to_all x2, waiting for transfers between devices, exchange(): return lax.all_to_all(pieces, axes, split_axis=0, concat_axis=0, tiled=True)  96.1 us
    all_to_all x3, blocking collectives, exchange(): return lax.all_to_all(pieces, axes, split_axis=0, concat_axis=0, tiled=True)  65.1 us
    pallas_call x1, Pallas kernels, layer(): pl.pallas_call(functools.partial(layer_kernel, take_steps, fan_one, fan_t...  16.6 us
    all_to_all x2, starting transfers between devices, exchange(): return lax.all_to_all(pieces, axes, split_axis=0, concat_axis=0, tiled=True)  11.4 us
    pallas_call x1, Pallas kernels, serve(): pl.pallas_call(serve_kernel, grid=(steps,), in_specs=[pl.BlockSpec((peers...  10.7 us
    dot_general x4, matrix products, dot(): return lax.dot_general(left, right, dims, preferred_element_type=F32)  9.2 us
    gather x1, local copies, waits for them, and re-layouts, body(): bias_turned = bias[jnp.asarray(order[0])][None, :]  8.81 us
    pallas_call x1, Pallas kernels, plan(): pl.pallas_call(lambda *refs: plan_kernel(devices, row_bits, far_lanes //...  4.78 us
  transfers between devices with their start and end apart: 2, of which 2 were waited for; matrix products, arithmetic and copies ran while one was open for 9% of the time, Pallas kernels for 0%

commit v1 on v0

v1 whole, which is shorter than its diff:
```python
import functools

import jax
import jax.numpy as jnp
import numpy as np
from jax import lax
from jax.experimental import pallas as pl
from jax.experimental.pallas import tpu as pltpu
from jax.sharding import Mesh
from jax.sharding import PartitionSpec as P

GX_GY = ("gx", "gy_0", "gy_1", "gy_2")
FAR_CAP = 9
NEAR_CAP = 2
SLOTS = 16
MAIN = 8
EXTRA = 4
PLAN_BLOCK = 256
BF16 = jnp.bfloat16
F32 = jnp.float32
INTERPRET = False

NN = (((1,), (0,)), ((), ()))
NT = (((1,), (1,)), ((), ()))


def dot(left, right, dims=NN):
    return lax.dot_general(left, right, dims, preferred_element_type=F32)


def round_up(value, step):
    return -(-value // step) * step


def plan_kernel(devices, row_bits, far_blocks, ids_ref, base_ref, group_ref, request_ref, groups_ref):
    lanes = ids_ref.shape[1]
    block = PLAN_BLOCK
    upper = (
        lax.broadcasted_iota(jnp.int32, (block, block), 0) < lax.broadcasted_iota(jnp.int32, (block, block), 1)
    ).astype(F32).astype(BF16)
    owner_at = lax.broadcasted_iota(jnp.int32, (devices, block), 0)
    slot_at = lax.broadcasted_iota(jnp.int32, (SLOTS, block), 0)
    carry = jnp.zeros((devices, 1), F32)
    request = jnp.zeros((devices, SLOTS), F32)
    groups = jnp.zeros((devices, SLOTS), F32)
    for at in range(lanes // block):
        here = slice(at * block, (at + 1) * block)
        ids = ids_ref[:, here]
        if at == far_blocks:
            carry = jnp.zeros((devices, 1), F32)
        match = (owner_at == lax.shift_right_arithmetic(ids, row_bits)).astype(F32)
        match_low = match.astype(BF16)
        before = dot(match_low, upper) + carry
        carry = carry + jnp.sum(match, axis=1, keepdims=True)
        rank = jnp.sum(match * before, axis=0, keepdims=True)
        slot = rank.astype(jnp.int32) + base_ref[:, here]
        placed = (slot_at == slot).astype(F32)
        local = ids & ((1 << row_bits) - 1)
        low = local & 31
        group = group_ref[:, here]
        group_low = group & 31
        request = request + dot(match_low, (placed * (local - low).astype(F32)).astype(BF16), NT)
        request = request + dot(match_low, (placed * low.astype(F32)).astype(BF16), NT)
        groups = groups + dot(match_low, (placed * (group - group_low).astype(F32)).astype(BF16), NT)
        groups = groups + dot(match_low, (placed * group_low.astype(F32)).astype(BF16), NT)
    request_ref[...] = request.astype(jnp.int32)
    groups_ref[...] = groups.astype(jnp.int32) - 1


def plan(near_ids, far_ids, devices, row_bits):
    seeds, fan_one = near_ids.shape
    fan_two = far_ids.shape[2]
    far_total = seeds * fan_one * fan_two
    near_total = seeds * fan_one
    far_lanes = round_up(far_total, PLAN_BLOCK)
    near_lanes = round_up(near_total, PLAN_BLOCK)
    ids = jnp.concatenate(
        [
            jnp.pad(far_ids.reshape(1, -1), ((0, 0), (0, far_lanes - far_total)), constant_values=-1),
            jnp.pad(near_ids.reshape(1, -1), ((0, 0), (0, near_lanes - near_total)), constant_values=-1),
        ],
        axis=1,
    )
    lanes = far_lanes + near_lanes
    base = np.zeros((1, lanes), np.int32)
    base[:, far_lanes:] = FAR_CAP
    group = np.zeros((1, lanes), np.int32)
    far_at = np.arange(far_total)
    group[0, :far_total] = (far_at // fan_two) % fan_one * seeds + far_at // (fan_one * fan_two) + 1
    near_at = np.arange(near_total)
    group[0, far_lanes : far_lanes + near_total] = near_at % fan_one * seeds + near_at // fan_one + 1
    out = jax.ShapeDtypeStruct((devices, SLOTS), jnp.int32)
    return pl.pallas_call(
        lambda *refs: plan_kernel(devices, row_bits, far_lanes // PLAN_BLOCK, *refs),
        out_shape=(out, out),
        name="plan",
        interpret=INTERPRET,
    )(ids, jnp.asarray(base), jnp.asarray(group))


def halves_swapped(rows):
    return pltpu.roll(rows, EXTRA, axis=1)


def serve_kernel(asked_ref, features_ref, out_ref):
    peers = asked_ref.shape[0]
    rows_dev, width = features_ref.shape
    half = width // 2
    asked = asked_ref[...].astype(F32)

    def rows_of(asked, places, first):
        count = asked.shape[0]
        wide = jnp.broadcast_to(asked, (count, MAIN, SLOTS)) if asked.shape[1] == 1 else asked
        lane = lax.broadcasted_iota(jnp.int32, (count, MAIN, SLOTS), 2)
        place = lax.broadcasted_iota(jnp.int32, (count, MAIN, SLOTS), 1)
        chosen = jnp.sum(jnp.where(lane == first + place % places, wide, 0.0), axis=2, keepdims=True)
        row_at = lax.broadcasted_iota(jnp.int32, (count, MAIN, rows_dev), 2).astype(F32)
        picks = (row_at == chosen).astype(F32).reshape(count * MAIN, rows_dev).astype(BF16)
        return dot(picks, features_ref[...])

    out_ref[:, :width] = rows_of(asked, MAIN, 0).astype(BF16)
    pairs = asked.reshape(peers // 2, 2, 1, SLOTS)
    upper = lax.broadcasted_iota(jnp.int32, (peers // 2, MAIN, SLOTS), 1) < EXTRA
    both = jnp.where(
        upper,
        jnp.broadcast_to(pairs[:, 0], (peers // 2, MAIN, SLOTS)),
        jnp.broadcast_to(pairs[:, 1], (peers // 2, MAIN, SLOTS)),
    )
    extra = rows_of(both, EXTRA, MAIN).reshape(peers // 2, MAIN, width)
    left, right = extra[:, :, :half], extra[:, :, half:]
    upper = lax.broadcasted_iota(jnp.int32, (peers // 2, MAIN, half), 1) < EXTRA
    even = jnp.where(upper, left, halves_swapped(right))
    odd = jnp.where(upper, halves_swapped(left), right)
    packed = jnp.stack([even, odd], axis=1).reshape(peers * MAIN, half)
    out_ref[:, width:] = packed.astype(BF16)


def serve(asked, features, steps=8):
    devices = asked.shape[0]
    rows_dev, width = features.shape
    peers = devices // steps
    payload = width + width // 2
    return pl.pallas_call(
        serve_kernel,
        grid=(steps,),
        in_specs=[
            pl.BlockSpec((peers, 1, SLOTS), lambda i: (i, 0, 0)),
            pl.BlockSpec((rows_dev, width), lambda i: (0, 0)),
        ],
        out_specs=pl.BlockSpec((peers * MAIN, payload), lambda i: (i, 0)),
        out_shape=jax.ShapeDtypeStruct((devices * MAIN, payload), BF16),
        name="serve",
        interpret=INTERPRET,
    )(asked, features)


def unpack_kernel(steps, fan_one, fan_two, rows_ref, main_ref, far_ref, near_ref, seed_ref, out_ref, far_acc, near_acc):
    step = pl.program_id(0)
    seeds, width = seed_ref.shape
    half = width // 2
    near_total = near_acc.shape[0]
    lanes = rows_ref.shape[0]

    @pl.when(step == 0)
    def _():
        far_acc[...] = jnp.zeros_like(far_acc)
        near_acc[...] = jnp.zeros_like(near_acc)

    def picks(groups):
        group_at = lax.broadcasted_iota(jnp.int32, (near_total, groups.shape[1]), 0)
        return (group_at == groups).astype(F32).astype(BF16)

    packed = rows_ref[:, width:].astype(F32).reshape(lanes // (2 * MAIN), 2, MAIN, half)
    even, odd = packed[:, 0], packed[:, 1]
    upper = lax.broadcasted_iota(jnp.int32, even.shape, 1) < EXTRA
    left = jnp.where(upper, even, halves_swapped(odd)).reshape(lanes // 2, half)
    right = jnp.where(upper, halves_swapped(even), odd).reshape(lanes // 2, half)
    extra = jnp.concatenate([left, right], axis=1).astype(BF16)
    far_acc[...] += dot(picks(main_ref[...]), rows_ref[:, :width]) + dot(picks(far_ref[...]), extra)
    near_acc[...] += dot(picks(near_ref[...]), extra)

    @pl.when(step == steps - 1)
    def _():
        out_ref[:near_total, :width] = near_acc[...].astype(BF16)
        out_ref[near_total:, :width] = seed_ref[...]
        out_ref[:near_total, width:] = (far_acc[...] / fan_two).astype(BF16)
        summed = near_acc[:seeds]
        for k in range(1, fan_one):
            summed = summed + near_acc[k * seeds : (k + 1) * seeds]
        out_ref[near_total:, width:] = (summed / fan_one).astype(BF16)


def unpack(rows, main, far, near, seed_x, fan_one, fan_two, steps=4):
    total, payload = rows.shape
    seeds, width = seed_x.shape
    lanes = total // steps
    near_total = seeds * fan_one
    return pl.pallas_call(
        functools.partial(unpack_kernel, steps, fan_one, fan_two),
        grid=(steps,),
        in_specs=[
            pl.BlockSpec((lanes, payload), lambda i: (i, 0)),
            pl.BlockSpec((1, lanes), lambda i: (0, i)),
            pl.BlockSpec((1, lanes // 2), lambda i: (0, i)),
            pl.BlockSpec((1, lanes // 2), lambda i: (0, i)),
            pl.BlockSpec((seeds, width), lambda i: (0, 0)),
        ],
        out_specs=pl.BlockSpec((near_total + seeds, 2 * width), lambda i: (0, 0)),
        out_shape=jax.ShapeDtypeStruct((near_total + seeds, 2 * width), BF16),
        scratch_shapes=[pltpu.VMEM((near_total, width), F32), pltpu.VMEM((near_total, width), F32)],
        name="unpack",
        interpret=INTERPRET,
    )(rows, main, far, near, seed_x)


def layer_kernel(fan_one, own_ref, pair_ref, self_ref, neigh_ref, bias_ref, spread_ref, embedded_ref, grad_ref):
    seeds = spread_ref.shape[0] // 2
    width = self_ref.shape[0]
    near_total = seeds * fan_one
    turned = []
    for at, rows_ref in enumerate((own_ref, pair_ref)):
        pre = dot(rows_ref[:, :width], self_ref[...]) + dot(rows_ref[:, width:], neigh_ref[...]) + bias_ref[...]
        hidden = jnp.maximum(pre, 0.0).astype(BF16).astype(F32)
        summed = hidden[near_total:]
        for k in range(fan_one):
            summed = summed + hidden[k * seeds : (k + 1) * seeds]
        here = slice(at * seeds, (at + 1) * seeds)
        embedded_ref[here] = (summed / (1 + fan_one)).astype(BF16)
        spread = spread_ref[here].astype(F32)
        delta = jnp.where(pre > 0, jnp.concatenate([spread] * (1 + fan_one), axis=0), 0.0)
        turned.append(delta.T.astype(BF16))
    grad_ref[:, : 2 * width] = (dot(turned[0], own_ref[...]) + dot(turned[1], pair_ref[...])).astype(BF16)
    ones = (lax.broadcasted_iota(jnp.int32, (own_ref.shape[0], 128), 1) == 0).astype(F32).astype(BF16)
    grad_ref[:, 2 * width :] = (dot(turned[0], ones) + dot(turned[1], ones)).astype(BF16)


def layer(own, pair, w_self, w_neigh, bias, spread, fan_one, steps=2):
    rows, both = own.shape
    width, hidden = w_self.shape
    part = hidden // steps
    seeds = spread.shape[0]
    whole = pl.BlockSpec((rows, both), lambda i: (0, 0))
    weights = pl.BlockSpec((width, part), lambda i: (0, i))
    return pl.pallas_call(
        functools.partial(layer_kernel, fan_one),
        grid=(steps,),
        in_specs=[
            whole,
            whole,
            weights,
            weights,
            pl.BlockSpec((1, part), lambda i: (0, i)),
            pl.BlockSpec((seeds, part), lambda i: (0, i)),
        ],
        out_specs=(
            pl.BlockSpec((seeds, part), lambda i: (0, i)),
            pl.BlockSpec((part, both + 128), lambda i: (i, 0)),
        ),
        out_shape=(
            jax.ShapeDtypeStruct((seeds, hidden), BF16),
            jax.ShapeDtypeStruct((hidden, both + 128), BF16),
        ),
        name="layer",
        interpret=INTERPRET,
    )(own, pair, w_self, w_neigh, bias, spread)


def exchange(pieces, axes):
    return lax.all_to_all(pieces, axes, split_axis=0, concat_axis=0, tiled=True)


def swapped(x):
    return lax.ppermute(x, "gy_2", [(0, 1), (1, 0)])


def slot_lanes(groups):
    main = groups[:, :MAIN].reshape(1, -1)
    extra = groups[:, MAIN : MAIN + EXTRA]
    at = jnp.arange(EXTRA, dtype=jnp.int32)[None, :]
    far = jnp.where(at < FAR_CAP - MAIN, extra, -1)
    near = jnp.where(at >= FAR_CAP - MAIN, extra, -1)
    return main, far.reshape(1, -1), near.reshape(1, -1)


def body(features, seed_rows, hop1_ids, hop2_ids, w_self, w_neigh, bias, cotangent):
    sizes = [lax.axis_size(a) for a in GX_GY]
    split_x, split_z, split_y, split_c = sizes
    devices = split_x * split_z * split_y * split_c
    rows_dev, width = features.shape
    row_bits = rows_dev.bit_length() - 1
    hidden = w_self.shape[1]
    seeds, fan_one = hop1_ids.shape
    fan_two = hop2_ids.shape[2]
    share = hidden // devices

    request, groups = plan(hop1_ids, hop2_ids, devices, row_bits)
    asked = exchange(request.reshape(devices, 1, SLOTS), GX_GY)
    served = serve(asked, features)
    rows = exchange(served.reshape(devices, MAIN, -1), GX_GY).reshape(devices * MAIN, -1)

    order = np.arange(hidden, dtype=np.int32).reshape(*sizes, share)
    order = jnp.asarray(np.transpose(order, (3, 0, 2, 1, 4)).reshape(split_c, hidden // split_c))
    core = lax.axis_index("gy_2")
    unit = lax.broadcasted_iota(jnp.int32, (hidden, hidden // split_c), 0)
    hit = unit == lax.dynamic_index_in_dim(order, core, 0)
    turn = hit.astype(BF16)
    turn_other = (unit == lax.dynamic_index_in_dim(order, 1 - core, 0)).astype(BF16)
    self_turned = dot(w_self, turn).astype(BF16)
    neigh_turned = dot(w_neigh, turn).astype(BF16)
    bias_turned = jnp.sum(jnp.where(hit, bias[:, None], 0.0), axis=0)[None, :]
    spread = (cotangent.astype(F32) / (1 + fan_one)).astype(BF16)
    spread_turned = dot(jnp.concatenate([spread, swapped(spread)], axis=0), turn).astype(BF16)
    seed_x = features[seed_rows]

    made = (self_turned, neigh_turned, bias_turned, spread_turned, seed_x, *slot_lanes(groups))
    rows, made = lax.optimization_barrier((rows, made))
    turned, seed_x, lanes = made[:4], made[4], made[5:]
    own = unpack(rows, *lanes, seed_x, fan_one, fan_two)
    embedded, grad = layer(own, swapped(own), *turned, fan_one)
    embedded = (dot(embedded[:seeds], turn, NT) + dot(swapped(embedded[seeds:]), turn_other, NT)).astype(BF16)

    pieces = exchange(grad.reshape(split_x * split_y, -1, grad.shape[-1]), ("gx", "gy_1"))
    grad = pieces.astype(F32).sum(axis=0).astype(BF16)
    grad = exchange(grad.reshape(split_z, share, -1), ("gy_0",)).astype(F32).sum(axis=0)
    return (embedded, grad[:, :width].T, grad[:, width : 2 * width].T, grad[:, 2 * width])


def solution(mesh):
    split = Mesh(mesh.devices.reshape(mesh.shape["gx"], 8, 4, 2), GX_GY)
    rows = P(GX_GY, None)
    in_specs = (rows, P(GX_GY), rows, P(GX_GY, None, None), P(), P(), P(), rows)
    out_specs = (rows, P(None, GX_GY), P(None, GX_GY), P(GX_GY))
    return jax.shard_map(body, mesh=split, in_specs=in_specs, out_specs=out_specs, check_vma=False)
```

time: 237 us -> 223 us (0.941)
  blocking collectives: 65.1 us -> 26.8 us
  waiting for transfers between devices: 96.1 us -> 131 us
  local copies, waits for them, and re-layouts: 16.4 us -> 8.6 us
  starting transfers between devices: 11.4 us -> 16.6 us
  Pallas kernels: 32.2 us -> 27.3 us
  other arithmetic: 5.49 us -> 2.01 us
    all_to_all x3 -> x1, blocking collectives: 65.1 us -> 26.8 us  [exchange(): return lax.all_to_all(pieces, axes, split_axis=0, concat_axis=0, tiled=True)]
    all_to_all x2 -> x3, waiting for transfers between devices: 96.1 us -> 127 us  [exchange(): return lax.all_to_all(pieces, axes, split_axis=0, concat_axis=0, tiled=True)]
    gather x1 -> x0, local copies, waits for them, and re-layouts: 8.81 us -> none  [body(): bias_turned = bias[jnp.asarray(order[0])][None, :]]
    all_to_all x2 -> x3, starting transfers between devices: 11.4 us -> 16.3 us  [exchange(): return lax.all_to_all(pieces, axes, split_axis=0, concat_axis=0, tiled=True)]
    ppermute x0 -> x3, waiting for transfers between devices: none -> 4.3 us  [swapped(): return lax.ppermute(x, 'gy_2', [(0, 1), (1, 0)])]
    pallas_call x1 -> x2, Pallas kernels: 16.6 us -> 13.3 us  [the longest x1 7.04 us: layer(): pl.pallas_call(functools.partial(layer_kernel, fan_one), grid=(steps,), i...]
    reduce_sum x3, other arithmetic: 4.62 us -> 1.26 us  [the longest x1 0.93 us: body(): bias_turned = jnp.sum(jnp.where(hit, bias[:, None], 0.0), axis=0)[None, :]]
    dot_general x4 -> x5, matrix products: 9.2 us -> 9.23 us  [dot(): return lax.dot_general(left, right, dims, preferred_element_type=F32)]
  transfers between devices with their start and end apart: 2 -> 6, of which waited for: 2 -> 5; matrix products, arithmetic and copies ran while one was open for 9% -> 6% of each run, Pallas kernels for 0% -> 0%
where the time goes in v1:
time: 223 us
  waiting for transfers between devices  131 us (59%)
  Pallas kernels  27.3 us (12%)
  blocking collectives  26.8 us (12%)
  starting transfers between devices  16.6 us (7%)
  matrix products  9.23 us (4%)
  local copies, waits for them, and re-layouts  8.6 us (4%)
    all_to_all x3, waiting for transfers between devices, exchange(): return lax.all_to_all(pieces, axes, split_axis=0, concat_axis=0, tiled=True)  127 us
    all_to_all x1, blocking collectives, exchange(): return lax.all_to_all(pieces, axes, split_axis=0, concat_axis=0, tiled=True)  26.8 us
    all_to_all x3, starting transfers between devices, exchange(): return lax.all_to_all(pieces, axes, split_axis=0, concat_axis=0, tiled=True)  16.3 us
    pallas_call x1, Pallas kernels, serve(): pl.pallas_call(serve_kernel, grid=(steps,), in_specs=[pl.BlockSpec((peers...  9.24 us
    dot_general x5, matrix products, dot(): return lax.dot_general(left, right, dims, preferred_element_type=F32)  9.23 us
    pallas_call x1, Pallas kernels, layer(): pl.pallas_call(functools.partial(layer_kernel, fan_one), grid=(steps,), i...  7.04 us
    pallas_call x1, Pallas kernels, unpack(): pl.pallas_call(functools.partial(unpack_kernel, steps, fan_one, fan_two),...  6.25 us
    pallas_call x1, Pallas kernels, plan(): pl.pallas_call(lambda *refs: plan_kernel(devices, row_bits, far_lanes //...  4.8 us
  transfers between devices with their start and end apart: 6, of which 5 were waited for; matrix products, arithmetic and copies ran while one was open for 6% of the time, Pallas kernels for 0%

profile of v1, /device:TPU:8, one launch (start us, length us, event | category | flops | bytes accessed | tf_op | source)
XLA Modules:
  0.0 222.9 jit_solution(18108199452918826411)
XLA Ops:
  0.6 0.0 copy-start
  0.6 0.9 copy.38
  1.5 0.1 reshape.50
  1.7 0.9 copy.37
  2.6 0.2 reshape.49
  2.8 0.6 fusion.21.refs_0_
  3.4 4.8 %plan.1 = (s32[256,16]{1,0:T(8,128)}, s32[256,16]{1,0:T(8,128)}) custom-call(s32[1,2304]{1,0:T(1,128)} %fusion.21.refs_0_, s32[1,2304]{1,0:T(1,128)} %constant.35.clone.refs_1_, s32[1,2304]{1,0:T(1,128)} %constant.36.clone.refs_2_), custom_call_target="tpu_custom_call" | custom-call | tf_op jit(solution)/shard_map/plan/pallas_call | solution.py:93
  8.2 26.8 %all_to_all.20.asked_ref = s32[256,1,16]{2,1,0:T(1,128)} all-to-all(s32[256,1,16]{2,1,0:T(1,128)} %bitcast.22), channel_id=1, replica_groups=mesh['gx'=4,'gy_0'=8,'gy_1'=4,'gy_2'=2] {'gx','gy_0','gy_1','gy_2'}, dimensions={0} | all-to-all | bytes 32768 | tf_op jit(solution)/shard_map/all_to_all | solution.py:269
  35.0 9.2 %serve.1 = bf16[2048,1152]{1,0:T(8,128)(2,1)} custom-call(s32[256,1,16]{2,1,0:T(1,128)} %all_to_all.20.asked_ref, bf16[1024,768]{1,0:T(8,128)(2,1)} %features_ref.1), custom_call_target="tpu_custom_call" | custom-call | tf_op jit(solution)/shard_map/serve/pallas_call | solution.py:143
  44.3 0.0 copy-start.3
  44.3 0.0 copy-start.7
  44.3 8.0 %all-to-all-start.1 = ((bf16[256,8,1152]{2,1,0:T(8,128)(2,1)}), bf16[256,8,1152]{2,1,0:T(8,128)(2,1)}, u32[]{:S(2)}, u32[]{:S(2)}) async-start(bf16[256,8,1152]{2,1,0:T(8,128)(2,1)} %bitcast.19), calls=%async_computation.1 | async-start | bytes 9437184 | tf_op jit(solution)/shard_map/all_to_all | solution.py:269
  52.3 0.0 copy-done.4
  52.4 0.2 collective-permute-start
  52.6 0.0 copy-done.9
  52.6 0.0 copy-done.1
  52.6 1.3 gather_fusion
  54.0 0.0 copy-done.3
  54.0 0.7 reshape.54.main_ref
  54.7 0.1 slice_select_fusion
  54.8 0.7 reshape.55.far_ref
  55.5 0.7 reshape.56.near_ref
  56.2 0.0 copy-done.7
  56.2 0.0 copy-start.8
  56.3 1.9 fusion.8.self_ref
  58.2 1.9 fusion.7.neigh_ref
  60.1 0.9 select_reduce_fusion
  61.0 0.0 collective-permute-done
  61.0 2.1 fusion.11.spread_ref
  63.1 98.5 %all-to-all-done.1 = bf16[256,8,1152]{2,1,0:T(8,128)(2,1)} async-done(((bf16[256,8,1152]{2,1,0:T(8,128)(2,1)}), bf16[256,8,1152]{2,1,0:T(8,128)(2,1)}, u32[]{:S(2)}, u32[]{:S(2)}) %all-to-all-start.1) | async-done | bytes 4718624 | tf_op jit(solution)/shard_map/all_to_all | solution.py:269
  161.6 6.2 %unpack.1.own_ref = bf16[384,1536]{1,0:T(8,128)(2,1)} custom-call(bf16[2048,1152]{1,0:T(8,128)(2,1)} %bitcast.2.rows_ref, s32[1,2048]{1,0:T(1,128)} %reshape.54.main_ref, s32[1,1024]{1,0:T(1,128)} %reshape.55.far_ref, s32[1,1024]{1,0:T(1,128)} %reshape.56.near_ref, bf16[64,768]{1,0:T(8,128)(2,1)} %gather_fusion), custom_call_target="tpu_custom_call" | custom-call | tf_op jit(solution)/shard_map/unpack/pallas_call | solution.py:198
  167.8 0.0 collective-permute-start.1
  167.8 3.1 %collective-permute-done.1.pair_ref = bf16[384,1536]{1,0:T(8,128)(2,1)S(1)} collective-permute-done((bf16[384,1536]{1,0:T(8,128)(2,1)}, bf16[384,1536]{1,0:T(8,128)(2,1)S(1)}, u32[]{:S(2)}, u32[]{:S(2)}) %collective-permute-start.1) | collective-permute-done | bytes 1179680 | tf_op jit(solution)/shard_map/ppermute | solution.py:273
  170.9 1.0 copy-done.2
  171.9 7.0 %layer.1 = (bf16[128,512]{1,0:T(8,128)(2,1)}, bf16[512,1664]{1,0:T(8,128)(2,1)}) custom-call(bf16[384,1536]{1,0:T(8,128)(2,1)} %unpack.1.own_ref, bf16[384,1536]{1,0:T(8,128)(2,1)} %copy-done.2, bf16[768,512]{1,0:T(8,128)(2,1)} %fusion.8.self_ref, bf16[768,512]{1,0:T(8,128)(2,1)} %fusion.7.neigh_ref, f32[1,512]{1,0:T(1,128)} %bitcast.23, ...), custom_call_target="tpu_custom_call" | custom-call | tf_op jit(solution)/shard_map/layer/pallas_call | solution.py:244
  179.0 4.9 %all-to-all-start.2 = ((bf16[16,32,1664]{2,1,0:T(8,128)(2,1)}), bf16[16,32,1664]{2,1,0:T(8,128)(2,1)S(1)}, u32[]{:S(2)}, u32[]{:S(2)}) async-start(bf16[16,32,1664]{2,1,0:T(8,128)(2,1)} %bitcast.20), calls=%async_computation.2 | async-start | bytes 3407872 | tf_op jit(solution)/shard_map/all_to_all | solution.py:269
  183.9 0.1 collective-permute-start.2
  184.0 1.2 collective-permute-done.2
  185.3 1.2 fusion.4
  186.5 22.1 %all-to-all-done.2 = bf16[16,32,1664]{2,1,0:T(8,128)(2,1)S(1)} async-done(((bf16[16,32,1664]{2,1,0:T(8,128)(2,1)}), bf16[16,32,1664]{2,1,0:T(8,128)(2,1)S(1)}, u32[]{:S(2)}, u32[]{:S(2)}) %all-to-all-start.2) | async-done | bytes 1703968 | tf_op jit(solution)/shard_map/all_to_all | solution.py:269
  208.5 0.3 reduce_sum.31
  208.8 0.7 reshape.58
  209.5 3.4 %all-to-all-start.3 = ((bf16[8,4,1664]{2,1,0:T(4,128)(2,1)}), bf16[8,4,1664]{2,1,0:T(4,128)(2,1)S(1)}, u32[]{:S(2)}, u32[]{:S(2)}) async-start(bf16[8,4,1664]{2,1,0:T(4,128)(2,1)} %reshape.58), calls=%async_computation.3 | async-start | bytes 212992 | tf_op jit(solution)/shard_map/all_to_all | solution.py:269
  212.8 2.1 fusion.10
  215.0 6.6 %all-to-all-done.3 = bf16[8,4,1664]{2,1,0:T(4,128)(2,1)S(1)} async-done(((bf16[8,4,1664]{2,1,0:T(4,128)(2,1)}), bf16[8,4,1664]{2,1,0:T(4,128)(2,1)S(1)}, u32[]{:S(2)}, u32[]{:S(2)}) %all-to-all-start.3) | async-done | bytes 106528 | tf_op jit(solution)/shard_map/all_to_all | solution.py:269
  221.6 0.1 convert_reduce_fusion
  221.6 0.6 slice_bitcast_fusion
  222.2 0.6 slice_reduce_fusion
  (16 shorter events, 0.1 us)
Async XLA Ops:
  0.6 55.6 %copy-start = (bf16[768,1024]{1,0:T(8,128)(2,1)S(1)}, bf16[768,1024]{1,0:T(8,128)(2,1)}, u32[]{:S(2)}) copy-start(bf16[768,1024]{1,0:T(8,128)(2,1)} %param.15) | copy-start | bytes 4718596
  44.3 8.1 %copy-start.4 = (bf16[64,1024]{1,0:T(8,128)(2,1)S(1)}, bf16[64,1024]{1,0:T(8,128)(2,1)}, u32[]{:S(2)}) copy-start(bf16[64,1024]{1,0:T(8,128)(2,1)} %param.18) | copy-start | bytes 393220
  44.3 8.3 %copy-start.9 = (s32[64]{0:T(128)S(1)}, s32[64]{0:T(128)}, u32[]{:S(2)}) copy-start(s32[64]{0:T(128)} %param.12) | copy-start | bytes 772
  44.3 8.3 %copy-start.1 = (bf16[1024,768]{1,0:T(8,128)(2,1)S(1)}, bf16[1024,768]{1,0:T(8,128)(2,1)}, u32[]{:S(2)}) copy-start(bf16[1024,768]{1,0:T(8,128)(2,1)} %features_ref.1) | copy-start | bytes 4718596
  44.3 9.7 %copy-start.3 = (s32[256,16]{1,0:T(8,128)S(1)}, s32[256,16]{1,0:T(8,128)}, u32[]{:S(2)}) copy-start(s32[256,16]{1,0:T(8,128)} %get-tuple-element.18) | copy-start | bytes 49156
  44.3 11.9 %copy-start.7 = (s32[2,512]{1,0:T(2,128)S(1)}, s32[2,512]{1,0:T(2,128)}, u32[]{:S(2)}) copy-start(s32[2,512]{1,0:T(2,128)} %constant.37.clone) | copy-start | bytes 12292
  44.3 117.3 %all-to-all-start.1 = ((bf16[256,8,1152]{2,1,0:T(8,128)(2,1)}), bf16[256,8,1152]{2,1,0:T(8,128)(2,1)}, u32[]{:S(2)}, u32[]{:S(2)}) async-start(bf16[256,8,1152]{2,1,0:T(8,128)(2,1)} %bitcast.19), calls=%async_computation.1 | async-start | bytes 9437184 | tf_op jit(solution)/shard_map/all_to_all | solution.py:269
  52.4 8.7 %collective-permute-start = (bf16[64,1024]{1,0:T(8,128)(2,1)S(1)}, bf16[64,1024]{1,0:T(8,128)(2,1)}, u32[]{:S(2)}, u32[]{:S(2)}) collective-permute-start(bf16[64,1024]{1,0:T(8,128)(2,1)S(1)} %multiply_convert_fusion), channel_id=1, source_target_pairs={{0,1},{1,0},{2,3},{3,2},{4,5},{5,4},{6,7},{7,6},{8,9},{9,8},{10,11... | collective-permute-start | bytes 393224 | tf_op jit(solution)/shard_map/ppermute | solution.py:273
  56.2 1.9 copy-start.8
  58.2 1.9 copy-start.6
  167.8 3.1 %collective-permute-start.1 = (bf16[384,1536]{1,0:T(8,128)(2,1)}, bf16[384,1536]{1,0:T(8,128)(2,1)S(1)}, u32[]{:S(2)}, u32[]{:S(2)}) collective-permute-start(bf16[384,1536]{1,0:T(8,128)(2,1)} %unpack.1.own_ref), channel_id=1, source_target_pairs={{0,1},{1,0},{2,3},{3,2},{4,5},{5,4},{6,7},{7,6},{8,9},{9,8},{10,11... | collective-permute-start | bytes 3538952 | tf_op jit(solution)/shard_map/ppermute | solution.py:273
  170.9 1.0 copy-start.2
  179.0 4.9 %copy-start.5 = (bf16[128,512]{1,0:T(8,128)(2,1)S(1)}, bf16[128,512]{1,0:T(8,128)(2,1)}, u32[]{:S(2)}) copy-start(bf16[128,512]{1,0:T(8,128)(2,1)} %get-tuple-element.28) | copy-start | bytes 393220
  179.0 29.6 %all-to-all-start.2 = ((bf16[16,32,1664]{2,1,0:T(8,128)(2,1)}), bf16[16,32,1664]{2,1,0:T(8,128)(2,1)S(1)}, u32[]{:S(2)}, u32[]{:S(2)}) async-start(bf16[16,32,1664]{2,1,0:T(8,128)(2,1)} %bitcast.20), calls=%async_computation.2 | async-start | bytes 3407872 | tf_op jit(solution)/shard_map/all_to_all | solution.py:269
  183.9 1.3 collective-permute-start.2
  209.5 12.1 %all-to-all-start.3 = ((bf16[8,4,1664]{2,1,0:T(4,128)(2,1)}), bf16[8,4,1664]{2,1,0:T(4,128)(2,1)S(1)}, u32[]{:S(2)}, u32[]{:S(2)}) async-start(bf16[8,4,1664]{2,1,0:T(4,128)(2,1)} %reshape.58), calls=%async_computation.3 | async-start | bytes 212992 | tf_op jit(solution)/shard_map/all_to_all | solution.py:269

commit v2 on v1

--- a/solution.py
+++ b/solution.py
@@ -13,8 +13,8 @@
 FAR_CAP = 9
 NEAR_CAP = 2
 SLOTS = 16
-MAIN = 8
-EXTRA = 4
+USED = FAR_CAP + NEAR_CAP
+LANES = 128
 PLAN_BLOCK = 256
 BF16 = jnp.bfloat16
 F32 = jnp.float32
@@ -41,8 +41,7 @@
     owner_at = lax.broadcasted_iota(jnp.int32, (devices, block), 0)
     slot_at = lax.broadcasted_iota(jnp.int32, (SLOTS, block), 0)
     carry = jnp.zeros((devices, 1), F32)
-    request = jnp.zeros((devices, SLOTS), F32)
-    groups = jnp.zeros((devices, SLOTS), F32)
+    found = jnp.zeros((4 * SLOTS, devices), F32)
     for at in range(lanes // block):
         here = slice(at * block, (at + 1) * block)
         ids = ids_ref[:, here]
@@ -59,11 +58,12 @@
         low = local & 31
         group = group_ref[:, here]
         group_low = group & 31
-        request = request + dot(match_low, (placed * (local - low).astype(F32)).astype(BF16), NT)
-        request = request + dot(match_low, (placed * low.astype(F32)).astype(BF16), NT)
-        groups = groups + dot(match_low, (placed * (group - group_low).astype(F32)).astype(BF16), NT)
-        groups = groups + dot(match_low, (placed * group_low.astype(F32)).astype(BF16), NT)
-    request_ref[...] = request.astype(jnp.int32)
+        values = (local - low, low, group - group_low, group_low)
+        stacked = jnp.concatenate([placed * value.astype(F32) for value in values], axis=0).astype(BF16)
+        found = found + dot(stacked, match_low, NT)
+    request = found[:SLOTS] + found[SLOTS : 2 * SLOTS]
+    groups = found[2 * SLOTS : 3 * SLOTS] + found[3 * SLOTS :]
+    request_ref[...] = request.T.astype(jnp.int32)
     groups_ref[...] = groups.astype(jnp.int32) - 1
 
 
@@ -89,95 +89,81 @@
     group[0, :far_total] = (far_at // fan_two) % fan_one * seeds + far_at // (fan_one * fan_two) + 1
     near_at = np.arange(near_total)
     group[0, far_lanes : far_lanes + near_total] = near_at % fan_one * seeds + near_at // fan_one + 1
-    out = jax.ShapeDtypeStruct((devices, SLOTS), jnp.int32)
+    out = (jax.ShapeDtypeStruct((devices, SLOTS), jnp.int32), jax.ShapeDtypeStruct((SLOTS, devices), jnp.int32))
     return pl.pallas_call(
         lambda *refs: plan_kernel(devices, row_bits, far_lanes // PLAN_BLOCK, *refs),
-        out_shape=(out, out),
+        out_shape=out,
         name="plan",
         interpret=INTERPRET,
     )(ids, jnp.asarray(base), jnp.asarray(group))
 
 
-def halves_swapped(rows):
-    return pltpu.roll(rows, EXTRA, axis=1)
-
-
-def serve_kernel(asked_ref, features_ref, out_ref):
+def serve_kernel(asked_ref, features_ref, out_ref, spread_out):
     peers = asked_ref.shape[0]
     rows_dev, width = features_ref.shape
-    half = width // 2
+    pieces = width // LANES
+    stride = USED * pieces
     asked = asked_ref[...].astype(F32)
-
-    def rows_of(asked, places, first):
-        count = asked.shape[0]
-        wide = jnp.broadcast_to(asked, (count, MAIN, SLOTS)) if asked.shape[1] == 1 else asked
-        lane = lax.broadcasted_iota(jnp.int32, (count, MAIN, SLOTS), 2)
-        place = lax.broadcasted_iota(jnp.int32, (count, MAIN, SLOTS), 1)
-        chosen = jnp.sum(jnp.where(lane == first + place % places, wide, 0.0), axis=2, keepdims=True)
-        row_at = lax.broadcasted_iota(jnp.int32, (count, MAIN, rows_dev), 2).astype(F32)
-        picks = (row_at == chosen).astype(F32).reshape(count * MAIN, rows_dev).astype(BF16)
-        return dot(picks, features_ref[...])
-
-    out_ref[:, :width] = rows_of(asked, MAIN, 0).astype(BF16)
-    pairs = asked.reshape(peers // 2, 2, 1, SLOTS)
-    upper = lax.broadcasted_iota(jnp.int32, (peers // 2, MAIN, SLOTS), 1) < EXTRA
-    both = jnp.where(
-        upper,
-        jnp.broadcast_to(pairs[:, 0], (peers // 2, MAIN, SLOTS)),
-        jnp.broadcast_to(pairs[:, 1], (peers // 2, MAIN, SLOTS)),
-    )
-    extra = rows_of(both, EXTRA, MAIN).reshape(peers // 2, MAIN, width)
-    left, right = extra[:, :, :half], extra[:, :, half:]
-    upper = lax.broadcasted_iota(jnp.int32, (peers // 2, MAIN, half), 1) < EXTRA
-    even = jnp.where(upper, left, halves_swapped(right))
-    odd = jnp.where(upper, halves_swapped(left), right)
-    packed = jnp.stack([even, odd], axis=1).reshape(peers * MAIN, half)
-    out_ref[:, width:] = packed.astype(BF16)
-
-
-def serve(asked, features, steps=8):
+    lane = lax.broadcasted_iota(jnp.int32, asked.shape, 1)
+    row_at = lax.broadcasted_iota(jnp.int32, (peers, rows_dev), 1).astype(F32)
+    picks = []
+    for slot in range(USED):
+        chosen = jnp.sum(jnp.where(lane == slot, asked, 0.0), axis=1, keepdims=True)
+        picks.append((row_at == chosen).astype(F32).astype(BF16))
+    found = dot(jnp.concatenate(picks, axis=0), features_ref[...])
+    for slot in range(USED):
+        rows = found[slot * peers : (slot + 1) * peers]
+        for piece in range(pieces):
+            spread_out[pl.ds(slot * pieces + piece, peers, stride=stride), :] = rows[:, piece * LANES : (piece + 1) * LANES]
+    out_ref[...] = spread_out[...].astype(BF16)
+
+
+def serve(asked, features, steps=4):
     devices = asked.shape[0]
     rows_dev, width = features.shape
     peers = devices // steps
-    payload = width + width // 2
+    rows = USED * width // LANES
     return pl.pallas_call(
         serve_kernel,
         grid=(steps,),
         in_specs=[
-            pl.BlockSpec((peers, 1, SLOTS), lambda i: (i, 0, 0)),
+            pl.BlockSpec((peers, SLOTS), lambda i: (i, 0)),
             pl.BlockSpec((rows_dev, width), lambda i: (0, 0)),
         ],
-        out_specs=pl.BlockSpec((peers * MAIN, payload), lambda i: (i, 0)),
-        out_shape=jax.ShapeDtypeStruct((devices * MAIN, payload), BF16),
+        out_specs=pl.BlockSpec((peers * rows, LANES), lambda i: (i, 0)),
+        out_shape=jax.ShapeDtypeStruct((devices * rows, LANES), BF16),
+        scratch_shapes=[pltpu.VMEM((peers * rows, LANES), F32)],
         name="serve",
         interpret=INTERPRET,
     )(asked, features)
 
 
-def unpack_kernel(steps, fan_one, fan_two, rows_ref, main_ref, far_ref, near_ref, seed_ref, out_ref, far_acc, near_acc):
+def unpack_kernel(steps, fan_one, fan_two, rows_ref, groups_ref, seed_ref, out_ref, wide, far_acc, near_acc):
     step = pl.program_id(0)
     seeds, width = seed_ref.shape
-    half = width // 2
+    pieces = width // LANES
+    stride = USED * pieces
     near_total = near_acc.shape[0]
-    lanes = rows_ref.shape[0]
+    peers = groups_ref.shape[1]
 
     @pl.when(step == 0)
     def _():
         far_acc[...] = jnp.zeros_like(far_acc)
         near_acc[...] = jnp.zeros_like(near_acc)
 
-    def picks(groups):
-        group_at = lax.broadcasted_iota(jnp.int32, (near_total, groups.shape[1]), 0)
-        return (group_at == groups).astype(F32).astype(BF16)
-
-    packed = rows_ref[:, width:].astype(F32).reshape(lanes // (2 * MAIN), 2, MAIN, half)
-    even, odd = packed[:, 0], packed[:, 1]
-    upper = lax.broadcasted_iota(jnp.int32, even.shape, 1) < EXTRA
-    left = jnp.where(upper, even, halves_swapped(odd)).reshape(lanes // 2, half)
-    right = jnp.where(upper, halves_swapped(even), odd).reshape(lanes // 2, half)
-    extra = jnp.concatenate([left, right], axis=1).astype(BF16)
-    far_acc[...] += dot(picks(main_ref[...]), rows_ref[:, :width]) + dot(picks(far_ref[...]), extra)
-    near_acc[...] += dot(picks(near_ref[...]), extra)
+    wide[...] = rows_ref[...].astype(F32)
+    group_at = lax.broadcasted_iota(jnp.int32, (near_total, peers), 0)
+
+    def taken(slots):
+        rows, picks = [], []
+        for slot in slots:
+            at = [wide[pl.ds(slot * pieces + piece, peers, stride=stride), :] for piece in range(pieces)]
+            rows.append(jnp.concatenate(at, axis=1).astype(BF16))
+            picks.append((group_at == groups_ref[slot : slot + 1, :]).astype(F32).astype(BF16))
+        return dot(jnp.concatenate(picks, axis=1), jnp.concatenate(rows, axis=0))
+
+    far_acc[...] += taken(range(FAR_CAP))
+    near_acc[...] += taken(range(FAR_CAP, USED))
 
     @pl.when(step == steps - 1)
     def _():
@@ -190,27 +176,29 @@
         out_ref[near_total:, width:] = (summed / fan_one).astype(BF16)
 
 
-def unpack(rows, main, far, near, seed_x, fan_one, fan_two, steps=4):
-    total, payload = rows.shape
+def unpack(rows, groups, seed_x, fan_one, fan_two, steps=2):
+    total = rows.shape[0]
     seeds, width = seed_x.shape
-    lanes = total // steps
+    peers = groups.shape[1] // steps
     near_total = seeds * fan_one
     return pl.pallas_call(
         functools.partial(unpack_kernel, steps, fan_one, fan_two),
         grid=(steps,),
         in_specs=[
-            pl.BlockSpec((lanes, payload), lambda i: (i, 0)),
-            pl.BlockSpec((1, lanes), lambda i: (0, i)),
-            pl.BlockSpec((1, lanes // 2), lambda i: (0, i)),
-            pl.BlockSpec((1, lanes // 2), lambda i: (0, i)),
+            pl.BlockSpec((total // steps, LANES), lambda i: (i, 0)),
+            pl.BlockSpec((groups.shape[0], peers), lambda i: (0, i)),
             pl.BlockSpec((seeds, width), lambda i: (0, 0)),
         ],
         out_specs=pl.BlockSpec((near_total + seeds, 2 * width), lambda i: (0, 0)),
         out_shape=jax.ShapeDtypeStruct((near_total + seeds, 2 * width), BF16),
-        scratch_shapes=[pltpu.VMEM((near_total, width), F32), pltpu.VMEM((near_total, width), F32)],
+        scratch_shapes=[
+            pltpu.VMEM((total // steps, LANES), F32),
+            pltpu.VMEM((near_total, width), F32),
+            pltpu.VMEM((near_total, width), F32),
+        ],
         name="unpack",
         interpret=INTERPRET,
-    )(rows, main, far, near, seed_x)
+    )(rows, groups, seed_x)
 
 
 def layer_kernel(fan_one, own_ref, pair_ref, self_ref, neigh_ref, bias_ref, spread_ref, embedded_ref, grad_ref):
@@ -273,15 +261,6 @@
     return lax.ppermute(x, "gy_2", [(0, 1), (1, 0)])
 
 
-def slot_lanes(groups):
-    main = groups[:, :MAIN].reshape(1, -1)
-    extra = groups[:, MAIN : MAIN + EXTRA]
-    at = jnp.arange(EXTRA, dtype=jnp.int32)[None, :]
-    far = jnp.where(at < FAR_CAP - MAIN, extra, -1)
-    near = jnp.where(at >= FAR_CAP - MAIN, extra, -1)
-    return main, far.reshape(1, -1), near.reshape(1, -1)
-
-
 def body(features, seed_rows, hop1_ids, hop2_ids, w_self, w_neigh, bias, cotangent):
     sizes = [lax.axis_size(a) for a in GX_GY]
     split_x, split_z, split_y, split_c = sizes
@@ -294,9 +273,9 @@
     share = hidden // devices
 
     request, groups = plan(hop1_ids, hop2_ids, devices, row_bits)
-    asked = exchange(request.reshape(devices, 1, SLOTS), GX_GY)
-    served = serve(asked, features)
-    rows = exchange(served.reshape(devices, MAIN, -1), GX_GY).reshape(devices * MAIN, -1)
+    asked = exchange(request.reshape(devices, 1, SLOTS), GX_GY).reshape(devices, SLOTS)
+    served = serve(asked, features).reshape(devices, -1, 2, LANES)
+    rows = exchange(served, GX_GY).reshape(-1, LANES)
 
     order = np.arange(hidden, dtype=np.int32).reshape(*sizes, share)
     order = jnp.asarray(np.transpose(order, (3, 0, 2, 1, 4)).reshape(split_c, hidden // split_c))
@@ -312,10 +291,10 @@
     spread_turned = dot(jnp.concatenate([spread, swapped(spread)], axis=0), turn).astype(BF16)
     seed_x = features[seed_rows]
 
-    made = (self_turned, neigh_turned, bias_turned, spread_turned, seed_x, *slot_lanes(groups))
+    made = (self_turned, neigh_turned, bias_turned, spread_turned, seed_x, groups)
     rows, made = lax.optimization_barrier((rows, made))
-    turned, seed_x, lanes = made[:4], made[4], made[5:]
-    own = unpack(rows, *lanes, seed_x, fan_one, fan_two)
+    turned, seed_x, lanes = made[:4], made[4], made[5]
+    own = unpack(rows, lanes, seed_x, fan_one, fan_two)
     embedded, grad = layer(own, swapped(own), *turned, fan_one)
     embedded = (dot(embedded[:seeds], turn, NT) + dot(swapped(embedded[seeds:]), turn_other, NT)).astype(BF16)
 

time: 223 us -> 211 us (0.946)
  waiting for transfers between devices: 131 us -> 125 us
  Pallas kernels: 27.3 us -> 23.2 us
    all_to_all x3, waiting for transfers between devices: 127 us -> 121 us  [exchange(): return lax.all_to_all(pieces, axes, split_axis=0, concat_axis=0, tiled=True)]
where the time goes in v2:
time: 211 us; the launch traced here: 210 us
  waiting for transfers between devices  125 us (59%)
  blocking collectives  26.9 us (13%)
  Pallas kernels  23.2 us (11%)
  starting transfers between devices  16.7 us (8%)
  matrix products  9.32 us (4%)
  local copies, waits for them, and re-layouts  6.46 us (3%)
    all_to_all x3, waiting for transfers between devices, exchange(): return lax.all_to_all(pieces, axes, split_axis=0, concat_axis=0, tiled=True)  121 us
    all_to_all x1, blocking collectives, exchange(): return lax.all_to_all(pieces, axes, split_axis=0, concat_axis=0, tiled=True)  26.9 us
    all_to_all x3, starting transfers between devices, exchange(): return lax.all_to_all(pieces, axes, split_axis=0, concat_axis=0, tiled=True)  16.4 us
    dot_general x5, matrix products, dot(): return lax.dot_general(left, right, dims, preferred_element_type=F32)  9.32 us
    pallas_call x1, Pallas kernels, serve(): pl.pallas_call(serve_kernel, grid=(steps,), in_specs=[pl.BlockSpec((peers...  8.33 us
    pallas_call x1, Pallas kernels, layer(): pl.pallas_call(functools.partial(layer_kernel, fan_one), grid=(steps,), i...  7.04 us
    pallas_call x1, Pallas kernels, unpack(): pl.pallas_call(functools.partial(unpack_kernel, steps, fan_one, fan_two),...  5.28 us
    ppermute x3, waiting for transfers between devices, swapped(): return lax.ppermute(x, 'gy_2', [(0, 1), (1, 0)])  4.3 us
  transfers between devices with their start and end apart: 6, of which 5 were waited for; matrix products, arithmetic and copies ran while one was open for 6% of the time, Pallas kernels for 0%

profile of v2, /device:TPU:8, one launch (start us, length us, event | category | flops | bytes accessed | tf_op | source)
XLA Modules:
  0.0 210.3 jit_solution(6667793052588091255)
XLA Ops:
  0.6 0.0 copy-start
  0.6 0.9 copy.46
  1.5 0.1 reshape.34
  1.7 0.9 copy.45
  2.6 0.2 reshape.33
  2.8 0.6 fusion.21.refs_0_
  3.4 2.6 %plan.1 = (s32[256,16]{1,0:T(8,128)}, s32[16,256]{1,0:T(8,128)}) custom-call(s32[1,2304]{1,0:T(1,128)} %fusion.21.refs_0_, s32[1,2304]{1,0:T(1,128)} %constant.34.clone.refs_1_, s32[1,2304]{1,0:T(1,128)} %constant.35.clone.refs_2_), custom_call_target="tpu_custom_call" | custom-call | tf_op jit(solution)/shard_map/plan/pallas_call | solution.py:93
  6.0 26.9 %all_to_all.20 = s32[256,1,16]{2,1,0:T(1,128)} all-to-all(s32[256,1,16]{2,1,0:T(1,128)} %bitcast.24), channel_id=1, replica_groups=mesh['gx'=4,'gy_0'=8,'gy_1'=4,'gy_2'=2] {'gx','gy_0','gy_1','gy_2'}, dimensions={0} | all-to-all | bytes 32768 | tf_op jit(solution)/shard_map/all_to_all | solution.py:257
  32.8 8.3 %serve.1 = bf16[16896,128]{1,0:T(8,128)(2,1)} custom-call(s32[256,16]{1,0:T(8,128)} %bitcast.23, bf16[1024,768]{1,0:T(8,128)(2,1)} %features_ref.1), custom_call_target="tpu_custom_call" | custom-call | tf_op jit(solution)/shard_map/serve/pallas_call | solution.py:126
  41.2 0.0 copy-start.3
  41.2 0.0 copy-start.8
  41.2 0.0 copy-start.6
  41.2 8.0 %all-to-all-start.1 = ((bf16[256,33,2,128]{3,2,1,0:T(2,128)(2,1)}), bf16[256,33,2,128]{3,2,1,0:T(2,128)(2,1)}, u32[]{:S(2)}, u32[]{:S(2)}) async-start(bf16[256,33,2,128]{3,2,1,0:T(2,128)(2,1)} %bitcast.21), calls=%async_computation.1 | async-start | bytes 8650752 | tf_op jit(solution)/shard_map/all_to_all | solution.py:257
  49.2 0.0 copy-done.3
  49.3 0.2 collective-permute-start
  49.5 0.0 copy-done.8
  49.5 0.0 copy-done.1
  49.5 1.4 gather_fusion
  50.9 0.0 copy-done.6
  50.9 0.0 copy-done
  50.9 0.0 copy-start.7
  50.9 2.0 fusion.8.self_ref
  52.9 0.0 copy-done.7
  52.9 1.9 fusion.7.neigh_ref
  54.8 0.0 copy-done.5
  54.8 0.9 select_reduce_fusion
  55.8 0.0 collective-permute-done
  55.8 2.1 fusion.11.spread_ref
  57.8 92.2 %all-to-all-done.1 = bf16[256,33,2,128]{3,2,1,0:T(2,128)(2,1)} async-done(((bf16[256,33,2,128]{3,2,1,0:T(2,128)(2,1)}), bf16[256,33,2,128]{3,2,1,0:T(2,128)(2,1)}, u32[]{:S(2)}, u32[]{:S(2)}) %all-to-all-start.1) | async-done | bytes 4325408 | tf_op jit(solution)/shard_map/all_to_all | solution.py:257
  150.0 5.3 %unpack.1.own_ref = bf16[384,1536]{1,0:T(8,128)(2,1)} custom-call(bf16[16896,128]{1,0:T(8,128)(2,1)} %bitcast.4.rows_ref, s32[16,256]{1,0:T(8,128)} %get-tuple-element.18.groups_ref, bf16[64,768]{1,0:T(8,128)(2,1)} %gather_fusion), custom_call_target="tpu_custom_call" | custom-call | tf_op jit(solution)/shard_map/unpack/pallas_call | solution.py:184
  155.3 0.0 collective-permute-start.1
  155.3 3.1 %collective-permute-done.1.pair_ref = bf16[384,1536]{1,0:T(8,128)(2,1)S(1)} collective-permute-done((bf16[384,1536]{1,0:T(8,128)(2,1)}, bf16[384,1536]{1,0:T(8,128)(2,1)S(1)}, u32[]{:S(2)}, u32[]{:S(2)}) %collective-permute-start.1) | collective-permute-done | bytes 1179680 | tf_op jit(solution)/shard_map/ppermute | solution.py:261
  158.4 1.0 copy-done.2
  159.4 7.0 %layer.1 = (bf16[128,512]{1,0:T(8,128)(2,1)}, bf16[512,1664]{1,0:T(8,128)(2,1)}) custom-call(bf16[384,1536]{1,0:T(8,128)(2,1)} %unpack.1.own_ref, bf16[384,1536]{1,0:T(8,128)(2,1)} %copy-done.2, bf16[768,512]{1,0:T(8,128)(2,1)} %fusion.8.self_ref, bf16[768,512]{1,0:T(8,128)(2,1)} %fusion.7.neigh_ref, f32[1,512]{1,0:T(1,128)} %bitcast.25, ...), custom_call_target="tpu_custom_call" | custom-call | tf_op jit(solution)/shard_map/layer/pallas_call | solution.py:232
  166.4 5.0 %all-to-all-start.2 = ((bf16[16,32,1664]{2,1,0:T(8,128)(2,1)}), bf16[16,32,1664]{2,1,0:T(8,128)(2,1)S(1)}, u32[]{:S(2)}, u32[]{:S(2)}) async-start(bf16[16,32,1664]{2,1,0:T(8,128)(2,1)} %bitcast.22), calls=%async_computation.2 | async-start | bytes 3407872 | tf_op jit(solution)/shard_map/all_to_all | solution.py:257
  171.4 0.0 copy-done.4
  171.4 0.1 collective-permute-start.2
  171.5 1.2 collective-permute-done.2
  172.7 1.2 fusion.4
  173.9 22.1 %all-to-all-done.2 = bf16[16,32,1664]{2,1,0:T(8,128)(2,1)S(1)} async-done(((bf16[16,32,1664]{2,1,0:T(8,128)(2,1)}), bf16[16,32,1664]{2,1,0:T(8,128)(2,1)S(1)}, u32[]{:S(2)}, u32[]{:S(2)}) %all-to-all-start.2) | async-done | bytes 1703968 | tf_op jit(solution)/shard_map/all_to_all | solution.py:257
  196.0 0.3 reduce_sum.31
  196.3 0.7 reshape.40
  196.9 3.4 %all-to-all-start.3 = ((bf16[8,4,1664]{2,1,0:T(4,128)(2,1)}), bf16[8,4,1664]{2,1,0:T(4,128)(2,1)S(1)}, u32[]{:S(2)}, u32[]{:S(2)}) async-start(bf16[8,4,1664]{2,1,0:T(4,128)(2,1)} %reshape.40), calls=%async_computation.3 | async-start | bytes 212992 | tf_op jit(solution)/shard_map/all_to_all | solution.py:257
  200.3 2.1 %fusion.10 = bf16[64,1024]{1,0:T(8,128)(2,1)} fusion(f32[64,1024]{1,0:T(8,128)} %fusion.4, s32[512]{0:T(512)S(1)} %bitcast.30, bf16[128,512]{1,0:T(8,128)(2,1)S(1)} %copy-done.4), kind=kOutput, calls=%fused_computation.14 | convolution fusion | flops 67764224 | bytes 460800 | tf_op jit(solution)/shard_map/dot_general | solution.py:28
  202.4 6.6 %all-to-all-done.3 = bf16[8,4,1664]{2,1,0:T(4,128)(2,1)S(1)} async-done(((bf16[8,4,1664]{2,1,0:T(4,128)(2,1)}), bf16[8,4,1664]{2,1,0:T(4,128)(2,1)S(1)}, u32[]{:S(2)}, u32[]{:S(2)}) %all-to-all-start.3) | async-done | bytes 106528 | tf_op jit(solution)/shard_map/all_to_all | solution.py:257
  209.0 0.1 convert_reduce_fusion
  209.1 0.6 slice_bitcast_fusion
  209.7 0.6 slice_reduce_fusion
  (9 shorter events, 0.1 us)
Async XLA Ops:
  0.6 50.2 %copy-start = (bf16[768,1024]{1,0:T(8,128)(2,1)S(1)}, bf16[768,1024]{1,0:T(8,128)(2,1)}, u32[]{:S(2)}) copy-start(bf16[768,1024]{1,0:T(8,128)(2,1)} %param.15) | copy-start | bytes 4718596
  41.2 8.1 %copy-start.3 = (bf16[64,1024]{1,0:T(8,128)(2,1)S(1)}, bf16[64,1024]{1,0:T(8,128)(2,1)}, u32[]{:S(2)}) copy-start(bf16[64,1024]{1,0:T(8,128)(2,1)} %param.18) | copy-start | bytes 393220
  41.2 8.3 %copy-start.8 = (s32[64]{0:T(128)S(1)}, s32[64]{0:T(128)}, u32[]{:S(2)}) copy-start(s32[64]{0:T(128)} %param.12) | copy-start | bytes 772
  41.2 8.3 %copy-start.1 = (bf16[1024,768]{1,0:T(8,128)(2,1)S(1)}, bf16[1024,768]{1,0:T(8,128)(2,1)}, u32[]{:S(2)}) copy-start(bf16[1024,768]{1,0:T(8,128)(2,1)} %features_ref.1) | copy-start | bytes 4718596
  41.2 9.7 %copy-start.6 = (s32[2,512]{1,0:T(2,128)S(1)}, s32[2,512]{1,0:T(2,128)}, u32[]{:S(2)}) copy-start(s32[2,512]{1,0:T(2,128)} %constant.36.clone) | copy-start | bytes 12292
  41.2 108.8 %all-to-all-start.1 = ((bf16[256,33,2,128]{3,2,1,0:T(2,128)(2,1)}), bf16[256,33,2,128]{3,2,1,0:T(2,128)(2,1)}, u32[]{:S(2)}, u32[]{:S(2)}) async-start(bf16[256,33,2,128]{3,2,1,0:T(2,128)(2,1)} %bitcast.21), calls=%async_computation.1 | async-start | bytes 8650752 | tf_op jit(solution)/shard_map/all_to_all | solution.py:257
  49.3 6.5 %collective-permute-start = (bf16[64,1024]{1,0:T(8,128)(2,1)S(1)}, bf16[64,1024]{1,0:T(8,128)(2,1)}, u32[]{:S(2)}, u32[]{:S(2)}) collective-permute-start(bf16[64,1024]{1,0:T(8,128)(2,1)S(1)} %multiply_convert_fusion), channel_id=1, source_target_pairs={{0,1},{1,0},{2,3},{3,2},{4,5},{5,4},{6,7},{7,6},{8,9},{9,8},{10,11... | collective-permute-start | bytes 393224 | tf_op jit(solution)/shard_map/ppermute | solution.py:261
  50.9 2.0 copy-start.7
  52.9 1.9 copy-start.5
  155.3 3.1 %collective-permute-start.1 = (bf16[384,1536]{1,0:T(8,128)(2,1)}, bf16[384,1536]{1,0:T(8,128)(2,1)S(1)}, u32[]{:S(2)}, u32[]{:S(2)}) collective-permute-start(bf16[384,1536]{1,0:T(8,128)(2,1)} %unpack.1.own_ref), channel_id=1, source_target_pairs={{0,1},{1,0},{2,3},{3,2},{4,5},{5,4},{6,7},{7,6},{8,9},{9,8},{10,11... | collective-permute-start | bytes 3538952 | tf_op jit(solution)/shard_map/ppermute | solution.py:261
  158.4 1.0 copy-start.2
  166.4 5.0 %copy-start.4 = (bf16[128,512]{1,0:T(8,128)(2,1)S(1)}, bf16[128,512]{1,0:T(8,128)(2,1)}, u32[]{:S(2)}) copy-start(bf16[128,512]{1,0:T(8,128)(2,1)} %get-tuple-element.24) | copy-start | bytes 393220
  166.4 29.6 %all-to-all-start.2 = ((bf16[16,32,1664]{2,1,0:T(8,128)(2,1)}), bf16[16,32,1664]{2,1,0:T(8,128)(2,1)S(1)}, u32[]{:S(2)}, u32[]{:S(2)}) async-start(bf16[16,32,1664]{2,1,0:T(8,128)(2,1)} %bitcast.22), calls=%async_computation.2 | async-start | bytes 3407872 | tf_op jit(solution)/shard_map/all_to_all | solution.py:257
  171.4 1.3 collective-permute-start.2
  196.9 12.1 %all-to-all-start.3 = ((bf16[8,4,1664]{2,1,0:T(4,128)(2,1)}), bf16[8,4,1664]{2,1,0:T(4,128)(2,1)S(1)}, u32[]{:S(2)}, u32[]{:S(2)}) async-start(bf16[8,4,1664]{2,1,0:T(4,128)(2,1)} %reshape.40), calls=%async_computation.3 | async-start | bytes 212992 | tf_op jit(solution)/shard_map/all_to_all | solution.py:257

commit v3 on v2

--- a/solution.py
+++ b/solution.py
@@ -32,35 +32,39 @@
     return -(-value // step) * step
 
 
-def plan_kernel(devices, row_bits, far_blocks, ids_ref, base_ref, group_ref, request_ref, groups_ref):
-    lanes = ids_ref.shape[1]
+def plan_kernel(devices, row_bits, far_ref, near_ref, request_ref, groups_ref):
+    fan_one, fan_two, seeds = far_ref.shape
     block = PLAN_BLOCK
     upper = (
         lax.broadcasted_iota(jnp.int32, (block, block), 0) < lax.broadcasted_iota(jnp.int32, (block, block), 1)
     ).astype(F32).astype(BF16)
     owner_at = lax.broadcasted_iota(jnp.int32, (devices, block), 0)
     slot_at = lax.broadcasted_iota(jnp.int32, (SLOTS, block), 0)
-    carry = jnp.zeros((devices, 1), F32)
+    lane = lax.broadcasted_iota(jnp.int32, (1, block), 1)
     found = jnp.zeros((4 * SLOTS, devices), F32)
-    for at in range(lanes // block):
-        here = slice(at * block, (at + 1) * block)
-        ids = ids_ref[:, here]
-        if at == far_blocks:
-            carry = jnp.zeros((devices, 1), F32)
-        match = (owner_at == lax.shift_right_arithmetic(ids, row_bits)).astype(F32)
-        match_low = match.astype(BF16)
-        before = dot(match_low, upper) + carry
-        carry = carry + jnp.sum(match, axis=1, keepdims=True)
-        rank = jnp.sum(match * before, axis=0, keepdims=True)
-        slot = rank.astype(jnp.int32) + base_ref[:, here]
-        placed = (slot_at == slot).astype(F32)
-        local = ids & ((1 << row_bits) - 1)
-        low = local & 31
-        group = group_ref[:, here]
-        group_low = group & 31
-        values = (local - low, low, group - group_low, group_low)
-        stacked = jnp.concatenate([placed * value.astype(F32) for value in values], axis=0).astype(BF16)
-        found = found + dot(stacked, match_low, NT)
+    far = [(k, far_ref[k, j : j + 1, :]) for k in range(fan_one) for j in range(fan_two)]
+    near = [(k, near_ref[k : k + 1, :]) for k in range(fan_one)]
+    for first, pieces in ((0, far), (FAR_CAP, near)):
+        carry = jnp.zeros((devices, 1), F32)
+        for at in range(0, len(pieces), block // seeds):
+            here = pieces[at : at + block // seeds]
+            rest = block // seeds - len(here)
+            ids = jnp.concatenate([ids for _, ids in here] + [jnp.full((1, seeds), -1, jnp.int32)] * rest, axis=1)
+            group = lane % seeds + 1
+            for place, (k, _) in enumerate(here):
+                group = group + jnp.where(lane // seeds == place, k * seeds, 0)
+            match = (owner_at == lax.shift_right_arithmetic(ids, row_bits)).astype(F32)
+            match_low = match.astype(BF16)
+            before = dot(match_low, upper) + carry
+            carry = carry + jnp.sum(match, axis=1, keepdims=True)
+            rank = jnp.sum(match * before, axis=0, keepdims=True)
+            placed = (slot_at == rank.astype(jnp.int32) + first).astype(F32)
+            local = ids & ((1 << row_bits) - 1)
+            low = local & 31
+            group_low = group & 31
+            values = (local - low, low, group - group_low, group_low)
+            stacked = jnp.concatenate([placed * value.astype(F32) for value in values], axis=0).astype(BF16)
+            found = found + dot(stacked, match_low, NT)
     request = found[:SLOTS] + found[SLOTS : 2 * SLOTS]
     groups = found[2 * SLOTS : 3 * SLOTS] + found[3 * SLOTS :]
     request_ref[...] = request.T.astype(jnp.int32)
@@ -68,34 +72,13 @@
 
 
 def plan(near_ids, far_ids, devices, row_bits):
-    seeds, fan_one = near_ids.shape
-    fan_two = far_ids.shape[2]
-    far_total = seeds * fan_one * fan_two
-    near_total = seeds * fan_one
-    far_lanes = round_up(far_total, PLAN_BLOCK)
-    near_lanes = round_up(near_total, PLAN_BLOCK)
-    ids = jnp.concatenate(
-        [
-            jnp.pad(far_ids.reshape(1, -1), ((0, 0), (0, far_lanes - far_total)), constant_values=-1),
-            jnp.pad(near_ids.reshape(1, -1), ((0, 0), (0, near_lanes - near_total)), constant_values=-1),
-        ],
-        axis=1,
-    )
-    lanes = far_lanes + near_lanes
-    base = np.zeros((1, lanes), np.int32)
-    base[:, far_lanes:] = FAR_CAP
-    group = np.zeros((1, lanes), np.int32)
-    far_at = np.arange(far_total)
-    group[0, :far_total] = (far_at // fan_two) % fan_one * seeds + far_at // (fan_one * fan_two) + 1
-    near_at = np.arange(near_total)
-    group[0, far_lanes : far_lanes + near_total] = near_at % fan_one * seeds + near_at // fan_one + 1
     out = (jax.ShapeDtypeStruct((devices, SLOTS), jnp.int32), jax.ShapeDtypeStruct((SLOTS, devices), jnp.int32))
     return pl.pallas_call(
-        lambda *refs: plan_kernel(devices, row_bits, far_lanes // PLAN_BLOCK, *refs),
+        functools.partial(plan_kernel, devices, row_bits),
         out_shape=out,
         name="plan",
         interpret=INTERPRET,
-    )(ids, jnp.asarray(base), jnp.asarray(group))
+    )(jnp.transpose(far_ids, (1, 2, 0)), jnp.transpose(near_ids))
 
 
 def serve_kernel(asked_ref, features_ref, out_ref, spread_out):
@@ -201,56 +184,82 @@
     )(rows, groups, seed_x)
 
 
-def layer_kernel(fan_one, own_ref, pair_ref, self_ref, neigh_ref, bias_ref, spread_ref, embedded_ref, grad_ref):
-    seeds = spread_ref.shape[0] // 2
+def layer_kernel(fan_one, rows_ref, self_ref, neigh_ref, bias_ref, spread_ref, *refs):
+    *earlier, embedded_ref, grad_ref = refs
+    seeds = spread_ref.shape[0]
     width = self_ref.shape[0]
     near_total = seeds * fan_one
-    turned = []
-    for at, rows_ref in enumerate((own_ref, pair_ref)):
-        pre = dot(rows_ref[:, :width], self_ref[...]) + dot(rows_ref[:, width:], neigh_ref[...]) + bias_ref[...]
-        hidden = jnp.maximum(pre, 0.0).astype(BF16).astype(F32)
-        summed = hidden[near_total:]
-        for k in range(fan_one):
-            summed = summed + hidden[k * seeds : (k + 1) * seeds]
-        here = slice(at * seeds, (at + 1) * seeds)
-        embedded_ref[here] = (summed / (1 + fan_one)).astype(BF16)
-        spread = spread_ref[here].astype(F32)
-        delta = jnp.where(pre > 0, jnp.concatenate([spread] * (1 + fan_one), axis=0), 0.0)
-        turned.append(delta.T.astype(BF16))
-    grad_ref[:, : 2 * width] = (dot(turned[0], own_ref[...]) + dot(turned[1], pair_ref[...])).astype(BF16)
-    ones = (lax.broadcasted_iota(jnp.int32, (own_ref.shape[0], 128), 1) == 0).astype(F32).astype(BF16)
-    grad_ref[:, 2 * width :] = (dot(turned[0], ones) + dot(turned[1], ones)).astype(BF16)
-
-
-def layer(own, pair, w_self, w_neigh, bias, spread, fan_one, steps=2):
-    rows, both = own.shape
+    pre = dot(rows_ref[:, :width], self_ref[...]) + dot(rows_ref[:, width:], neigh_ref[...]) + bias_ref[...]
+    hidden = jnp.maximum(pre, 0.0).astype(BF16).astype(F32)
+    summed = hidden[near_total:]
+    for k in range(fan_one):
+        summed = summed + hidden[k * seeds : (k + 1) * seeds]
+    embedded_ref[...] = (summed / (1 + fan_one)).astype(BF16)
+    spread = spread_ref[...].astype(F32)
+    delta = jnp.where(pre > 0, jnp.concatenate([spread] * (1 + fan_one), axis=0), 0.0)
+    turned = delta.T.astype(BF16)
+    ones = (lax.broadcasted_iota(jnp.int32, (rows_ref.shape[0], LANES), 1) == 0).astype(F32).astype(BF16)
+    for start, part in ((0, rows_ref[...]), (2 * width, ones)):
+        here = slice(start, start + part.shape[1])
+        grad = dot(turned, part)
+        for ref in earlier:
+            grad = grad + ref[:, here]
+        grad_ref[:, here] = grad.astype(grad_ref.dtype)
+
+
+def layer(rows, w_self, w_neigh, bias, spread, fan_one, earlier=(), steps=2):
+    count, both = rows.shape
     width, hidden = w_self.shape
     part = hidden // steps
     seeds = spread.shape[0]
-    whole = pl.BlockSpec((rows, both), lambda i: (0, 0))
     weights = pl.BlockSpec((width, part), lambda i: (0, i))
+    grads = pl.BlockSpec((part, both + LANES), lambda i: (i, 0))
     return pl.pallas_call(
         functools.partial(layer_kernel, fan_one),
         grid=(steps,),
         in_specs=[
-            whole,
-            whole,
+            pl.BlockSpec((count, both), lambda i: (0, 0)),
             weights,
             weights,
             pl.BlockSpec((1, part), lambda i: (0, i)),
             pl.BlockSpec((seeds, part), lambda i: (0, i)),
+            *[grads for _ in earlier],
         ],
-        out_specs=(
-            pl.BlockSpec((seeds, part), lambda i: (0, i)),
-            pl.BlockSpec((part, both + 128), lambda i: (i, 0)),
-        ),
+        out_specs=(pl.BlockSpec((seeds, part), lambda i: (0, i)), grads),
         out_shape=(
             jax.ShapeDtypeStruct((seeds, hidden), BF16),
-            jax.ShapeDtypeStruct((hidden, both + 128), BF16),
+            jax.ShapeDtypeStruct((hidden, both + LANES), BF16 if earlier else F32),
         ),
-        name="layer",
-        interpret=INTERPRET,
-    )(own, pair, w_self, w_neigh, bias, spread)
+        name="layer_second" if earlier else "layer_first",
+        interpret=INTERPRET,
+    )(rows, w_self, w_neigh, bias, spread, *earlier)
+
+
+def last_kernel(pieces_ref, self_ref, neigh_ref, bias_ref):
+    share, width = self_ref.shape
+    summed = pieces_ref[0].astype(F32)
+    for at in range(1, pieces_ref.shape[0]):
+        summed = summed + pieces_ref[at].astype(F32)
+    self_ref[...] = summed[:, :width]
+    neigh_ref[...] = summed[:, width : 2 * width]
+    square = (share, share)
+    here = lax.broadcasted_iota(jnp.int32, square, 0) == lax.broadcasted_iota(jnp.int32, square, 1)
+    column = jnp.broadcast_to(summed[:, 2 * width : 2 * width + 1], square)
+    bias_ref[...] = jnp.sum(jnp.where(here, column, 0.0), axis=0, keepdims=True)
+
+
+def last(pieces, width):
+    share = pieces.shape[1]
+    return pl.pallas_call(
+        last_kernel,
+        out_shape=(
+            jax.ShapeDtypeStruct((share, width), F32),
+            jax.ShapeDtypeStruct((share, width), F32),
+            jax.ShapeDtypeStruct((1, share), F32),
+        ),
+        name="last",
+        interpret=INTERPRET,
+    )(pieces)
 
 
 def exchange(pieces, axes):
@@ -295,13 +304,17 @@
     rows, made = lax.optimization_barrier((rows, made))
     turned, seed_x, lanes = made[:4], made[4], made[5]
     own = unpack(rows, lanes, seed_x, fan_one, fan_two)
-    embedded, grad = layer(own, swapped(own), *turned, fan_one)
-    embedded = (dot(embedded[:seeds], turn, NT) + dot(swapped(embedded[seeds:]), turn_other, NT)).astype(BF16)
+    *turned, spread_turned = turned
+    pair = swapped(own)
+    embedded_own, grad = layer(own, *turned, spread_turned[:seeds], fan_one)
+    embedded_pair, grad = layer(pair, *turned, spread_turned[seeds:], fan_one, (grad,))
+    embedded = (dot(embedded_own, turn, NT) + dot(swapped(embedded_pair), turn_other, NT)).astype(BF16)
 
     pieces = exchange(grad.reshape(split_x * split_y, -1, grad.shape[-1]), ("gx", "gy_1"))
     grad = pieces.astype(F32).sum(axis=0).astype(BF16)
-    grad = exchange(grad.reshape(split_z, share, -1), ("gy_0",)).astype(F32).sum(axis=0)
-    return (embedded, grad[:, :width].T, grad[:, width : 2 * width].T, grad[:, 2 * width])
+    pieces = exchange(grad.reshape(split_z, share, -1), ("gy_0",))
+    grad_self, grad_neigh, grad_bias = last(pieces, width)
+    return (embedded, grad_self.T, grad_neigh.T, grad_bias.reshape(-1))
 
 
 def solution(mesh):

time: 211 us -> 213 us (level)
  Pallas kernels: 23.2 us -> 30.9 us
    pallas_call x1 -> x2, Pallas kernels: 7.04 us -> 13.1 us  [layer(): pl.pallas_call(functools.partial(layer_kernel, fan_one), grid=(steps,), i...]
    ppermute x3, waiting for transfers between devices: 4.3 us -> 0.01 us  [swapped(): return lax.ppermute(x, 'gy_2', [(0, 1), (1, 0)])]
    all_to_all x3, waiting for transfers between devices: 121 us -> 124 us  [exchange(): return lax.all_to_all(pieces, axes, split_axis=0, concat_axis=0, tiled=True)]
  transfers between devices with their start and end apart: 6 -> 6, of which waited for: 5 -> 3; matrix products, arithmetic and copies ran while one was open for 6% -> 5% of each run, Pallas kernels for 0% -> 3%
where the time goes in v3:
time: 213 us
  waiting for transfers between devices  124 us (58%)
  Pallas kernels  30.9 us (15%)
  blocking collectives  26.9 us (13%)
  starting transfers between devices  16.8 us (8%)
  matrix products  7.71 us (4%)
  local copies, waits for them, and re-layouts  4.43 us (2%)
    all_to_all x3, waiting for transfers between devices, exchange(): return lax.all_to_all(pieces, axes, split_axis=0, concat_axis=0, tiled=True)  124 us
    all_to_all x1, blocking collectives, exchange(): return lax.all_to_all(pieces, axes, split_axis=0, concat_axis=0, tiled=True)  26.9 us
    all_to_all x3, starting transfers between devices, exchange(): return lax.all_to_all(pieces, axes, split_axis=0, concat_axis=0, tiled=True)  16.4 us
    pallas_call x2, Pallas kernels, layer(): pl.pallas_call(functools.partial(layer_kernel, fan_one), grid=(steps,), i...  13.1 us
    pallas_call x1, Pallas kernels, serve(): pl.pallas_call(serve_kernel, grid=(steps,), in_specs=[pl.BlockSpec((peers...  8.33 us
    dot_general x5, matrix products, dot(): return lax.dot_general(left, right, dims, preferred_element_type=F32)  7.71 us
    pallas_call x1, Pallas kernels, unpack(): pl.pallas_call(functools.partial(unpack_kernel, steps, fan_one, fan_two),...  5.31 us
  transfers between devices with their start and end apart: 6, of which 3 were waited for; matrix products, arithmetic and copies ran while one was open for 5% of the time, Pallas kernels for 3%

profile of v3, /device:TPU:8, one launch (start us, length us, event | category | flops | bytes accessed | tf_op | source)
XLA Modules:
  0.0 213.0 jit_solution(16561962831973229150)
XLA Ops:
  0.6 0.0 copy-start
  0.6 2.7 %plan.1 = (s32[256,16]{1,0:T(8,128)}, s32[16,256]{1,0:T(8,128)}) custom-call(s32[5,5,64]{2,1,0:T(8,128)} %bitcast.27, s32[5,64]{1,0:T(8,128)} %bitcast.35), custom_call_target="tpu_custom_call" | custom-call | tf_op jit(solution)/shard_map/plan/pallas_call | solution.py:76
  3.4 26.9 %all_to_all.20 = s32[256,1,16]{2,1,0:T(1,128)} all-to-all(s32[256,1,16]{2,1,0:T(1,128)} %bitcast.26), channel_id=1, replica_groups=mesh['gx'=4,'gy_0'=8,'gy_1'=4,'gy_2'=2] {'gx','gy_0','gy_1','gy_2'}, dimensions={0} | all-to-all | bytes 32768 | tf_op jit(solution)/shard_map/all_to_all | solution.py:266
  30.2 8.3 %serve.1 = bf16[16896,128]{1,0:T(8,128)(2,1)} custom-call(s32[256,16]{1,0:T(8,128)} %bitcast.25, bf16[1024,768]{1,0:T(8,128)(2,1)} %features_ref.1), custom_call_target="tpu_custom_call" | custom-call | tf_op jit(solution)/shard_map/serve/pallas_call | solution.py:109
  38.6 0.0 copy-start.4
  38.6 0.0 copy-start.10
  38.6 0.0 copy-start.1
  38.6 0.0 copy-start.6
  38.6 8.0 %all-to-all-start.1 = ((bf16[256,33,2,128]{3,2,1,0:T(2,128)(2,1)}), bf16[256,33,2,128]{3,2,1,0:T(2,128)(2,1)}, u32[]{:S(2)}, u32[]{:S(2)}) async-start(bf16[256,33,2,128]{3,2,1,0:T(2,128)(2,1)} %bitcast.23), calls=%async_computation.1 | async-start | bytes 8650752 | tf_op jit(solution)/shard_map/all_to_all | solution.py:266
  46.6 0.0 copy-done.4
  46.7 0.2 collective-permute-start
  46.9 0.0 copy-done.10
  46.9 0.0 copy-done.1
  46.9 1.3 gather_fusion
  48.2 0.0 copy-done.6
  48.3 0.0 copy-done
  48.3 0.0 copy-start.7
  48.3 2.0 fusion.8.self_ref
  50.3 0.0 copy-done.7
  50.3 1.9 fusion.7.neigh_ref
  52.2 0.0 copy-done.5
  52.2 0.9 select_reduce_fusion
  53.1 0.0 collective-permute-done
  53.1 0.5 fusion.11
  53.6 93.8 %all-to-all-done.1 = bf16[256,33,2,128]{3,2,1,0:T(2,128)(2,1)} async-done(((bf16[256,33,2,128]{3,2,1,0:T(2,128)(2,1)}), bf16[256,33,2,128]{3,2,1,0:T(2,128)(2,1)}, u32[]{:S(2)}, u32[]{:S(2)}) %all-to-all-start.1) | async-done | bytes 4325408 | tf_op jit(solution)/shard_map/all_to_all | solution.py:266
  147.4 5.3 %unpack.1.rows_ref = bf16[384,1536]{1,0:T(8,128)(2,1)} custom-call(bf16[16896,128]{1,0:T(8,128)(2,1)} %bitcast.6.rows_ref, s32[16,256]{1,0:T(8,128)} %get-tuple-element.23.groups_ref, bf16[64,768]{1,0:T(8,128)(2,1)} %gather_fusion), custom_call_target="tpu_custom_call" | custom-call | tf_op jit(solution)/shard_map/unpack/pallas_call | solution.py:167
  152.7 0.0 collective-permute-start.1
  152.7 0.7 fusion.21
  153.4 6.4 %layer_first.1 = (bf16[64,512]{1,0:T(8,128)(2,1)}, f32[512,1664]{1,0:T(8,128)}) custom-call(bf16[384,1536]{1,0:T(8,128)(2,1)} %unpack.1.rows_ref, bf16[768,512]{1,0:T(8,128)(2,1)} %fusion.8.self_ref, bf16[768,512]{1,0:T(8,128)(2,1)} %fusion.7.neigh_ref, f32[1,512]{1,0:T(1,128)} %bitcast.28, bf16[64,512]{1,0:T(8,128)(2,1)} %get-tuple-element.37.spread_ref), custom_call_target="tpu_custom_call" | custom-call | tf_op jit(solution)/shard_map/layer_first/pallas_call | solution.py:217
  159.8 0.0 collective-permute-done.1.rows_ref
  159.8 0.0 copy-start.2
  159.8 1.0 copy-done.2
  160.8 6.7 %layer_second.1 = (bf16[64,512]{1,0:T(8,128)(2,1)}, bf16[512,1664]{1,0:T(8,128)(2,1)}) custom-call(bf16[384,1536]{1,0:T(8,128)(2,1)} %copy-done.2, bf16[768,512]{1,0:T(8,128)(2,1)} %fusion.8.self_ref, bf16[768,512]{1,0:T(8,128)(2,1)} %fusion.7.neigh_ref, f32[1,512]{1,0:T(1,128)} %bitcast.29, bf16[64,512]{1,0:T(8,128)(2,1)} %get-tuple-element.36.spread_ref, ...), custom_call_target="tpu_custom_call" | custom-call | tf_op jit(solution)/shard_map/layer_second/pallas_call | solution.py:217
  167.5 0.0 copy-start.8
  167.5 5.1 %all-to-all-start.2 = ((bf16[16,32,1664]{2,1,0:T(8,128)(2,1)}), bf16[16,32,1664]{2,1,0:T(8,128)(2,1)S(1)}, u32[]{:S(2)}, u32[]{:S(2)}) async-start(bf16[16,32,1664]{2,1,0:T(8,128)(2,1)} %bitcast.24), calls=%async_computation.2 | async-start | bytes 3407872 | tf_op jit(solution)/shard_map/all_to_all | solution.py:266
  172.6 0.0 copy-done.8
  172.6 0.1 collective-permute-start.2
  172.7 0.0 copy-done.9
  172.7 1.2 fusion
  173.9 23.9 %all-to-all-done.2 = bf16[16,32,1664]{2,1,0:T(8,128)(2,1)S(1)} async-done(((bf16[16,32,1664]{2,1,0:T(8,128)(2,1)}), bf16[16,32,1664]{2,1,0:T(8,128)(2,1)S(1)}, u32[]{:S(2)}, u32[]{:S(2)}) %all-to-all-start.2) | async-done | bytes 1703968 | tf_op jit(solution)/shard_map/all_to_all | solution.py:266
  197.8 0.2 reduce_sum.22
  198.1 0.7 reshape.35
  198.7 3.4 %all-to-all-start.3 = ((bf16[8,4,1664]{2,1,0:T(4,128)(2,1)}), bf16[8,4,1664]{2,1,0:T(4,128)(2,1)S(1)}, u32[]{:S(2)}, u32[]{:S(2)}) async-start(bf16[8,4,1664]{2,1,0:T(4,128)(2,1)} %reshape.35), calls=%async_computation.3 | async-start | bytes 212992 | tf_op jit(solution)/shard_map/all_to_all | solution.py:266
  202.1 0.0 collective-permute-done.2
  202.1 2.1 %fusion.10 = bf16[64,1024]{1,0:T(8,128)(2,1)} fusion(f32[64,1024]{1,0:T(8,128)} %fusion, bf16[64,512]{1,0:T(8,128)(2,1)S(1)} %collective-permute-done.2, s32[512]{0:T(512)S(1)} %bitcast.36), kind=kOutput, calls=%fused_computation.14 | convolution fusion | flops 67764224 | bytes 460800 | tf_op jit(solution)/shard_map/dot_general | solution.py:28
  204.3 6.6 %all-to-all-done.3.pieces_ref = bf16[8,4,1664]{2,1,0:T(4,128)(2,1)S(1)} async-done(((bf16[8,4,1664]{2,1,0:T(4,128)(2,1)}), bf16[8,4,1664]{2,1,0:T(4,128)(2,1)S(1)}, u32[]{:S(2)}, u32[]{:S(2)}) %all-to-all-start.3) | async-done | bytes 106528 | tf_op jit(solution)/shard_map/all_to_all | solution.py:266
  210.8 0.6 copy-done.3
  211.5 1.5 last.1
  (7 shorter events, 0.0 us)
Async XLA Ops:
  0.6 47.6 %copy-start = (bf16[768,1024]{1,0:T(8,128)(2,1)S(1)}, bf16[768,1024]{1,0:T(8,128)(2,1)}, u32[]{:S(2)}) copy-start(bf16[768,1024]{1,0:T(8,128)(2,1)} %param.13) | copy-start | bytes 4718596
  38.6 8.1 %copy-start.4 = (bf16[64,1024]{1,0:T(8,128)(2,1)S(1)}, bf16[64,1024]{1,0:T(8,128)(2,1)}, u32[]{:S(2)}) copy-start(bf16[64,1024]{1,0:T(8,128)(2,1)} %param.16) | copy-start | bytes 393220
  38.6 8.3 %copy-start.10 = (s32[64]{0:T(128)S(1)}, s32[64]{0:T(128)}, u32[]{:S(2)}) copy-start(s32[64]{0:T(128)} %param.10) | copy-start | bytes 772
  38.6 8.3 %copy-start.1 = (bf16[1024,768]{1,0:T(8,128)(2,1)S(1)}, bf16[1024,768]{1,0:T(8,128)(2,1)}, u32[]{:S(2)}) copy-start(bf16[1024,768]{1,0:T(8,128)(2,1)} %features_ref.1) | copy-start | bytes 4718596
  38.6 9.7 %copy-start.6 = (s32[2,512]{1,0:T(2,128)S(1)}, s32[2,512]{1,0:T(2,128)}, u32[]{:S(2)}) copy-start(s32[2,512]{1,0:T(2,128)} %constant.28.clone) | copy-start | bytes 12292
  38.6 108.8 %all-to-all-start.1 = ((bf16[256,33,2,128]{3,2,1,0:T(2,128)(2,1)}), bf16[256,33,2,128]{3,2,1,0:T(2,128)(2,1)}, u32[]{:S(2)}, u32[]{:S(2)}) async-start(bf16[256,33,2,128]{3,2,1,0:T(2,128)(2,1)} %bitcast.23), calls=%async_computation.1 | async-start | bytes 8650752 | tf_op jit(solution)/shard_map/all_to_all | solution.py:266
  46.7 6.4 %collective-permute-start = (bf16[64,1024]{1,0:T(8,128)(2,1)S(1)}, bf16[64,1024]{1,0:T(8,128)(2,1)S(1)}, u32[]{:S(2)}, u32[]{:S(2)}) collective-permute-start(bf16[64,1024]{1,0:T(8,128)(2,1)S(1)} %multiply_convert_fusion), channel_id=1, source_target_pairs={{0,1},{1,0},{2,3},{3,2},{4,5},{5,4},{6,7},{7,6},{8,9},{9,8},{10,11... | collective-permute-start | bytes 393224 | tf_op jit(solution)/shard_map/ppermute | solution.py:270
  48.3 2.0 copy-start.7
  50.3 1.9 copy-start.5
  152.7 7.1 %collective-permute-start.1 = (bf16[384,1536]{1,0:T(8,128)(2,1)}, bf16[384,1536]{1,0:T(8,128)(2,1)S(1)}, u32[]{:S(2)}, u32[]{:S(2)}) collective-permute-start(bf16[384,1536]{1,0:T(8,128)(2,1)} %unpack.1.rows_ref), channel_id=1, source_target_pairs={{0,1},{1,0},{2,3},{3,2},{4,5},{5,4},{6,7},{7,6},{8,9},{9,8},{10,11... | collective-permute-start | bytes 3538952 | tf_op jit(solution)/shard_map/ppermute | solution.py:270
  159.8 1.1 copy-start.2
  167.5 5.1 %copy-start.8 = (bf16[64,512]{1,0:T(8,128)(2,1)S(1)}, bf16[64,512]{1,0:T(8,128)(2,1)}, u32[]{:S(2)}) copy-start(bf16[64,512]{1,0:T(8,128)(2,1)} %get-tuple-element.31) | copy-start | bytes 196612
  167.5 5.2 %copy-start.9 = (bf16[64,512]{1,0:T(8,128)(2,1)S(1)}, bf16[64,512]{1,0:T(8,128)(2,1)}, u32[]{:S(2)}) copy-start(bf16[64,512]{1,0:T(8,128)(2,1)} %get-tuple-element.29) | copy-start | bytes 196612
  167.5 30.3 %all-to-all-start.2 = ((bf16[16,32,1664]{2,1,0:T(8,128)(2,1)}), bf16[16,32,1664]{2,1,0:T(8,128)(2,1)S(1)}, u32[]{:S(2)}, u32[]{:S(2)}) async-start(bf16[16,32,1664]{2,1,0:T(8,128)(2,1)} %bitcast.24), calls=%async_computation.2 | async-start | bytes 3407872 | tf_op jit(solution)/shard_map/all_to_all | solution.py:266
  172.6 29.5 %collective-permute-start.2 = (bf16[64,512]{1,0:T(8,128)(2,1)S(1)}, bf16[64,512]{1,0:T(8,128)(2,1)S(1)}, u32[]{:S(2)}, u32[]{:S(2)}) collective-permute-start(bf16[64,512]{1,0:T(8,128)(2,1)S(1)} %copy-done.8), channel_id=1, source_target_pairs={{0,1},{1,0},{2,3},{3,2},{4,5},{5,4},{6,7},{7,6},{8,9},{9,8},{10,11... | collective-permute-start | bytes 196616 | tf_op jit(solution)/shard_map/ppermute | solution.py:270
  198.7 12.1 %all-to-all-start.3 = ((bf16[8,4,1664]{2,1,0:T(4,128)(2,1)}), bf16[8,4,1664]{2,1,0:T(4,128)(2,1)S(1)}, u32[]{:S(2)}, u32[]{:S(2)}) async-start(bf16[8,4,1664]{2,1,0:T(4,128)(2,1)} %reshape.35), calls=%async_computation.3 | async-start | bytes 212992 | tf_op jit(solution)/shard_map/all_to_all | solution.py:266
  210.8 0.6 copy-start.3

commit v4 on v3

--- a/solution.py
+++ b/solution.py
@@ -19,6 +19,7 @@
 BF16 = jnp.bfloat16
 F32 = jnp.float32
 INTERPRET = False
+KERNEL_VMEM = 40 << 20
 
 NN = (((1,), (0,)), ((), ()))
 NT = (((1,), (1,)), ((), ()))
@@ -28,11 +29,22 @@
     return lax.dot_general(left, right, dims, preferred_element_type=F32)
 
 
-def round_up(value, step):
-    return -(-value // step) * step
-
-
-def plan_kernel(devices, row_bits, far_ref, near_ref, request_ref, groups_ref):
+ON_CHIP = pl.BlockSpec(memory_space=pltpu.VMEM)
+
+
+def on_chip(x):
+    return pltpu.with_memory_space_constraint(x, pltpu.VMEM)
+
+
+def plan_kernel(
+    devices, row_bits, far_hbm, near_hbm, features_hbm, request_ref, groups_ref, held_ref, far_ref, near_ref, arrived
+):
+    pairs = ((far_hbm, far_ref), (near_hbm, near_ref), (features_hbm, held_ref))
+    copies = [pltpu.make_async_copy(*pair, arrived.at[at]) for at, pair in enumerate(pairs)]
+    for copy in copies:
+        copy.start()
+    for copy in copies[:2]:
+        copy.wait()
     fan_one, fan_two, seeds = far_ref.shape
     block = PLAN_BLOCK
     upper = (
@@ -69,16 +81,31 @@
     groups = found[2 * SLOTS : 3 * SLOTS] + found[3 * SLOTS :]
     request_ref[...] = request.T.astype(jnp.int32)
     groups_ref[...] = groups.astype(jnp.int32) - 1
-
-
-def plan(near_ids, far_ids, devices, row_bits):
-    out = (jax.ShapeDtypeStruct((devices, SLOTS), jnp.int32), jax.ShapeDtypeStruct((SLOTS, devices), jnp.int32))
+    copies[2].wait()
+
+
+def plan(near_ids, far_ids, features, devices, row_bits):
+    out = (
+        jax.ShapeDtypeStruct((devices, SLOTS), jnp.int32),
+        jax.ShapeDtypeStruct((SLOTS, devices), jnp.int32),
+        pltpu.VMEM(features.shape, features.dtype),
+    )
+    far_ids, near_ids = jnp.transpose(far_ids, (1, 2, 0)), jnp.transpose(near_ids)
+    inputs = [pltpu.with_memory_space_constraint(x, pltpu.HBM) for x in (far_ids, near_ids, features)]
     return pl.pallas_call(
         functools.partial(plan_kernel, devices, row_bits),
+        in_specs=[pl.BlockSpec(memory_space=pltpu.HBM)] * 3,
+        out_specs=(ON_CHIP,) * 3,
         out_shape=out,
+        scratch_shapes=[
+            pltpu.VMEM(far_ids.shape, jnp.int32),
+            pltpu.VMEM(near_ids.shape, jnp.int32),
+            pltpu.SemaphoreType.DMA((3,)),
+        ],
+        compiler_params=pltpu.CompilerParams(vmem_limit_bytes=KERNEL_VMEM),
         name="plan",
         interpret=INTERPRET,
-    )(jnp.transpose(far_ids, (1, 2, 0)), jnp.transpose(near_ids))
+    )(*inputs)
 
 
 def serve_kernel(asked_ref, features_ref, out_ref, spread_out):
@@ -111,14 +138,15 @@
         grid=(steps,),
         in_specs=[
             pl.BlockSpec((peers, SLOTS), lambda i: (i, 0)),
-            pl.BlockSpec((rows_dev, width), lambda i: (0, 0)),
+            ON_CHIP,
         ],
         out_specs=pl.BlockSpec((peers * rows, LANES), lambda i: (i, 0)),
-        out_shape=jax.ShapeDtypeStruct((devices * rows, LANES), BF16),
+        out_shape=pltpu.HBM((devices * rows, LANES), BF16),
         scratch_shapes=[pltpu.VMEM((peers * rows, LANES), F32)],
+        compiler_params=pltpu.CompilerParams(vmem_limit_bytes=KERNEL_VMEM),
         name="serve",
         interpret=INTERPRET,
-    )(asked, features)
+    )(asked, on_chip(features))
 
 
 def unpack_kernel(steps, fan_one, fan_two, rows_ref, groups_ref, seed_ref, out_ref, wide, far_acc, near_acc):
@@ -172,20 +200,20 @@
             pl.BlockSpec((groups.shape[0], peers), lambda i: (0, i)),
             pl.BlockSpec((seeds, width), lambda i: (0, 0)),
         ],
-        out_specs=pl.BlockSpec((near_total + seeds, 2 * width), lambda i: (0, 0)),
-        out_shape=jax.ShapeDtypeStruct((near_total + seeds, 2 * width), BF16),
+        out_specs=ON_CHIP,
+        out_shape=pltpu.VMEM((near_total + seeds, 2 * width), BF16),
         scratch_shapes=[
             pltpu.VMEM((total // steps, LANES), F32),
             pltpu.VMEM((near_total, width), F32),
             pltpu.VMEM((near_total, width), F32),
         ],
+        compiler_params=pltpu.CompilerParams(vmem_limit_bytes=KERNEL_VMEM),
         name="unpack",
         interpret=INTERPRET,
     )(rows, groups, seed_x)
 
 
-def layer_kernel(fan_one, rows_ref, self_ref, neigh_ref, bias_ref, spread_ref, *refs):
-    *earlier, embedded_ref, grad_ref = refs
+def forward(fan_one, rows_ref, self_ref, neigh_ref, bias_ref, spread_ref, embedded_ref):
     seeds = spread_ref.shape[0]
     width = self_ref.shape[0]
     near_total = seeds * fan_one
@@ -196,70 +224,84 @@
         summed = summed + hidden[k * seeds : (k + 1) * seeds]
     embedded_ref[...] = (summed / (1 + fan_one)).astype(BF16)
     spread = spread_ref[...].astype(F32)
-    delta = jnp.where(pre > 0, jnp.concatenate([spread] * (1 + fan_one), axis=0), 0.0)
-    turned = delta.T.astype(BF16)
-    ones = (lax.broadcasted_iota(jnp.int32, (rows_ref.shape[0], LANES), 1) == 0).astype(F32).astype(BF16)
-    for start, part in ((0, rows_ref[...]), (2 * width, ones)):
-        here = slice(start, start + part.shape[1])
-        grad = dot(turned, part)
-        for ref in earlier:
-            grad = grad + ref[:, here]
-        grad_ref[:, here] = grad.astype(grad_ref.dtype)
-
-
-def layer(rows, w_self, w_neigh, bias, spread, fan_one, earlier=(), steps=2):
+    return jnp.where(pre > 0, jnp.concatenate([spread] * (1 + fan_one), axis=0), 0.0).T
+
+
+def first_kernel(fan_one, part, rows_ref, self_ref, neigh_ref, bias_ref, spread_ref, embedded_ref, turned_ref):
+    here = pl.ds(pl.multiple_of(pl.program_id(0) * part, part), part)
+    turned = forward(fan_one, rows_ref, self_ref, neigh_ref, bias_ref, spread_ref, embedded_ref)
+    turned_ref[here, :] = turned.astype(BF16)
+
+
+def second_kernel(
+    fan_one, part, rows_ref, self_ref, neigh_ref, bias_ref, spread_ref, own_ref, turned_ref, embedded_ref, grad_ref, both
+):
+    count, columns = own_ref.shape
+    here = pl.ds(pl.multiple_of(pl.program_id(0) * part, part), part)
+
+    @pl.when(pl.program_id(0) == 0)
+    def _():
+        both[:count] = own_ref[...]
+        both[count:] = rows_ref[...]
+
+    pair = forward(fan_one, rows_ref, self_ref, neigh_ref, bias_ref, spread_ref, embedded_ref)
+    turned = jnp.concatenate([turned_ref[here, :], pair.astype(BF16)], axis=1)
+    grad_ref[:, :columns] = dot(turned, both[...]).astype(BF16)
+    summed = jnp.sum(turned.astype(F32), axis=1, keepdims=True)
+    grad_ref[:, columns:] = jnp.broadcast_to(summed, (part, LANES)).astype(BF16)
+
+
+def layer(rows, w_self, w_neigh, bias, spread, fan_one, own=(), steps=2):
     count, both = rows.shape
     width, hidden = w_self.shape
     part = hidden // steps
     seeds = spread.shape[0]
     weights = pl.BlockSpec((width, part), lambda i: (0, i))
-    grads = pl.BlockSpec((part, both + LANES), lambda i: (i, 0))
-    return pl.pallas_call(
-        functools.partial(layer_kernel, fan_one),
+    half = pl.BlockSpec((seeds, part), lambda i: (0, i))
+    if own:
+        last_spec = pl.BlockSpec((part, both + LANES), lambda i: (i, 0))
+        last_shape = pltpu.HBM((hidden, both + LANES), BF16)
+    else:
+        last_spec = ON_CHIP
+        last_shape = pltpu.VMEM((hidden, count), BF16)
+    return pl.pallas_call(
+        functools.partial(second_kernel if own else first_kernel, fan_one, part),
         grid=(steps,),
         in_specs=[
-            pl.BlockSpec((count, both), lambda i: (0, 0)),
+            ON_CHIP,
             weights,
             weights,
             pl.BlockSpec((1, part), lambda i: (0, i)),
-            pl.BlockSpec((seeds, part), lambda i: (0, i)),
-            *[grads for _ in earlier],
-        ],
-        out_specs=(pl.BlockSpec((seeds, part), lambda i: (0, i)), grads),
-        out_shape=(
-            jax.ShapeDtypeStruct((seeds, hidden), BF16),
-            jax.ShapeDtypeStruct((hidden, both + LANES), BF16 if earlier else F32),
-        ),
-        name="layer_second" if earlier else "layer_first",
-        interpret=INTERPRET,
-    )(rows, w_self, w_neigh, bias, spread, *earlier)
-
-
-def last_kernel(pieces_ref, self_ref, neigh_ref, bias_ref):
-    share, width = self_ref.shape
+            half,
+            *[ON_CHIP for _ in own],
+        ],
+        out_specs=(half, last_spec),
+        out_shape=(jax.ShapeDtypeStruct((seeds, hidden), BF16), last_shape),
+        scratch_shapes=[pltpu.VMEM((2 * count, both), BF16)] if own else [],
+        compiler_params=pltpu.CompilerParams(vmem_limit_bytes=KERNEL_VMEM),
+        name="layer_second" if own else "layer_first",
+        interpret=INTERPRET,
+    )(on_chip(rows), w_self, w_neigh, bias, spread, *[on_chip(x) for x in own])
+
+
+def sum_kernel(pieces_ref, out_ref):
     summed = pieces_ref[0].astype(F32)
     for at in range(1, pieces_ref.shape[0]):
         summed = summed + pieces_ref[at].astype(F32)
-    self_ref[...] = summed[:, :width]
-    neigh_ref[...] = summed[:, width : 2 * width]
-    square = (share, share)
-    here = lax.broadcasted_iota(jnp.int32, square, 0) == lax.broadcasted_iota(jnp.int32, square, 1)
-    column = jnp.broadcast_to(summed[:, 2 * width : 2 * width + 1], square)
-    bias_ref[...] = jnp.sum(jnp.where(here, column, 0.0), axis=0, keepdims=True)
-
-
-def last(pieces, width):
-    share = pieces.shape[1]
-    return pl.pallas_call(
-        last_kernel,
-        out_shape=(
-            jax.ShapeDtypeStruct((share, width), F32),
-            jax.ShapeDtypeStruct((share, width), F32),
-            jax.ShapeDtypeStruct((1, share), F32),
-        ),
-        name="last",
-        interpret=INTERPRET,
-    )(pieces)
+    out_ref[...] = summed.reshape(out_ref.shape).astype(BF16)
+
+
+def sum_pieces(pieces, groups):
+    _, rows, columns = pieces.shape
+    return pl.pallas_call(
+        sum_kernel,
+        in_specs=[ON_CHIP],
+        out_specs=ON_CHIP,
+        out_shape=pltpu.VMEM((groups, rows // groups, columns), BF16),
+        compiler_params=pltpu.CompilerParams(vmem_limit_bytes=KERNEL_VMEM),
+        name="sum_pieces",
+        interpret=INTERPRET,
+    )(on_chip(pieces))
 
 
 def exchange(pieces, axes):
@@ -281,9 +323,9 @@
     fan_two = hop2_ids.shape[2]
     share = hidden // devices
 
-    request, groups = plan(hop1_ids, hop2_ids, devices, row_bits)
+    request, groups, held = plan(hop1_ids, hop2_ids, features, devices, row_bits)
     asked = exchange(request.reshape(devices, 1, SLOTS), GX_GY).reshape(devices, SLOTS)
-    served = serve(asked, features).reshape(devices, -1, 2, LANES)
+    served = serve(asked, held).reshape(devices, -1, 2, LANES)
     rows = exchange(served, GX_GY).reshape(-1, LANES)
 
     order = np.arange(hidden, dtype=np.int32).reshape(*sizes, share)
@@ -297,24 +339,22 @@
     neigh_turned = dot(w_neigh, turn).astype(BF16)
     bias_turned = jnp.sum(jnp.where(hit, bias[:, None], 0.0), axis=0)[None, :]
     spread = (cotangent.astype(F32) / (1 + fan_one)).astype(BF16)
-    spread_turned = dot(jnp.concatenate([spread, swapped(spread)], axis=0), turn).astype(BF16)
+    spread_own = dot(spread, turn).astype(BF16)
+    spread_pair = dot(swapped(spread), turn).astype(BF16)
     seed_x = features[seed_rows]
 
-    made = (self_turned, neigh_turned, bias_turned, spread_turned, seed_x, groups)
+    made = (self_turned, neigh_turned, bias_turned, spread_own, spread_pair, seed_x, groups)
     rows, made = lax.optimization_barrier((rows, made))
-    turned, seed_x, lanes = made[:4], made[4], made[5]
+    *turned, spread_own, spread_pair, seed_x, lanes = made
     own = unpack(rows, lanes, seed_x, fan_one, fan_two)
-    *turned, spread_turned = turned
     pair = swapped(own)
-    embedded_own, grad = layer(own, *turned, spread_turned[:seeds], fan_one)
-    embedded_pair, grad = layer(pair, *turned, spread_turned[seeds:], fan_one, (grad,))
+    embedded_own, delta_own = layer(own, *turned, spread_own, fan_one)
+    embedded_pair, grad = layer(pair, *turned, spread_pair, fan_one, (own, delta_own))
     embedded = (dot(embedded_own, turn, NT) + dot(swapped(embedded_pair), turn_other, NT)).astype(BF16)
 
     pieces = exchange(grad.reshape(split_x * split_y, -1, grad.shape[-1]), ("gx", "gy_1"))
-    grad = pieces.astype(F32).sum(axis=0).astype(BF16)
-    pieces = exchange(grad.reshape(split_z, share, -1), ("gy_0",))
-    grad_self, grad_neigh, grad_bias = last(pieces, width)
-    return (embedded, grad_self.T, grad_neigh.T, grad_bias.reshape(-1))
+    grad = exchange(sum_pieces(pieces, split_z), ("gy_0",)).astype(F32).sum(axis=0)
+    return (embedded, grad[:, :width].T, grad[:, width : 2 * width].T, grad[:, 2 * width])
 
 
 def solution(mesh):

time: 213 us -> 201 us (0.944)
  Pallas kernels: 30.9 us -> 19.8 us
    pallas_call x4, Pallas kernels: 17.3 us -> 8.63 us  [the longest x2 5.66 us: layer(): pl.pallas_call(functools.partial(second_kernel if own else first_kernel,...]
    dot_general x5 -> x6, matrix products: 7.71 us -> 7.26 us  [dot(): return lax.dot_general(left, right, dims, preferred_element_type=F32)]
  transfers between devices with their start and end apart: 6 -> 6, of which waited for: 3 -> 4; matrix products, arithmetic and copies ran while one was open for 5% -> 4% of each run, Pallas kernels for 3% -> 1%
where the time goes in v4:
time: 201 us; the launch traced here: 200 us
  waiting for transfers between devices  126 us (63%)
  blocking collectives  26.4 us (13%)
  Pallas kernels  19.8 us (10%)
  starting transfers between devices  16.7 us (8%)
  matrix products  7.26 us (4%)
  local copies, waits for them, and re-layouts  2.35 us (1%)
    all_to_all x3, waiting for transfers between devices, exchange(): return lax.all_to_all(pieces, axes, split_axis=0, concat_axis=0, tiled=True)  125 us
    all_to_all x1, blocking collectives, exchange(): return lax.all_to_all(pieces, axes, split_axis=0, concat_axis=0, tiled=True)  26.4 us
    all_to_all x3, starting transfers between devices, exchange(): return lax.all_to_all(pieces, axes, split_axis=0, concat_axis=0, tiled=True)  16.3 us
    dot_general x6, matrix products, dot(): return lax.dot_general(left, right, dims, preferred_element_type=F32)  7.26 us
    pallas_call x1, Pallas kernels, serve(): pl.pallas_call(serve_kernel, grid=(steps,), in_specs=[pl.BlockSpec((peers...  6.9 us
    pallas_call x2, Pallas kernels, layer(): pl.pallas_call(functools.partial(second_kernel if own else first_kernel,...  5.66 us
    pallas_call x1, Pallas kernels, unpack(): pl.pallas_call(functools.partial(unpack_kernel, steps, fan_one, fan_two),...  4.24 us
  transfers between devices with their start and end apart: 6, of which 4 were waited for; matrix products, arithmetic and copies ran while one was open for 4% of the time, Pallas kernels for 1%

profile of v4, /device:TPU:8, one launch (start us, length us, event | category | flops | bytes accessed | tf_op | source)
XLA Modules:
  0.0 200.4 jit_solution(4512008823574263017)
XLA Ops:
  0.6 0.0 copy-start
  0.6 2.1 %plan.1 = (s32[256,16]{1,0:T(8,128)S(1)}, s32[16,256]{1,0:T(8,128)S(1)}, bf16[1024,768]{1,0:T(8,128)(2,1)S(1)}) custom-call(s32[5,5,64]{2,1,0:T(8,128)} %bitcast.31, s32[5,64]{1,0:T(8,128)} %bitcast.38, bf16[1024,768]{1,0:T(8,128)(2,1)} %features_hbm.1), custom_call_target="tpu_custom_call" | custom-call | tf_op jit(solution)/shard_map/plan/pallas_call | solution.py:95
  2.7 26.4 %all_to_all.20 = s32[256,1,16]{2,1,0:T(1,128)S(1)} all-to-all(s32[256,1,16]{2,1,0:T(1,128)S(1)} %bitcast.26), channel_id=1, replica_groups=mesh['gx'=4,'gy_0'=8,'gy_1'=4,'gy_2'=2] {'gx','gy_0','gy_1','gy_2'}, dimensions={0} | all-to-all | bytes 32768 | tf_op jit(solution)/shard_map/all_to_all | solution.py:308
  29.1 6.9 %serve.1 = bf16[16896,128]{1,0:T(8,128)(2,1)} custom-call(s32[256,16]{1,0:T(8,128)S(1)} %bitcast.25, bf16[1024,768]{1,0:T(8,128)(2,1)S(1)} %get-tuple-element.20.features_ref), custom_call_target="tpu_custom_call" | custom-call | tf_op jit(solution)/shard_map/serve/pallas_call | solution.py:136
  36.0 0.0 copy-start.2
  36.0 0.0 copy-start.6
  36.0 0.0 copy-start.1
  36.1 0.0 copy-start.4
  36.1 8.1 %all-to-all-start.1 = ((bf16[256,33,2,128]{3,2,1,0:T(2,128)(2,1)}), bf16[256,33,2,128]{3,2,1,0:T(2,128)(2,1)}, u32[]{:S(2)}, u32[]{:S(2)}) async-start(bf16[256,33,2,128]{3,2,1,0:T(2,128)(2,1)} %bitcast.29), calls=%async_computation.1 | async-start | bytes 8650752 | tf_op jit(solution)/shard_map/all_to_all | solution.py:308
  44.1 0.0 copy-done.2
  44.1 0.7 multiply_convert_fusion
  44.8 0.1 collective-permute-start
  45.0 0.0 copy-done.6
  45.0 0.0 copy-done.1
  45.0 0.7 gather_fusion
  45.7 0.0 copy-done.4
  45.7 0.5 fusion.12.spread_ref
  46.2 0.0 copy-done
  46.2 0.0 copy-start.5
  46.2 1.0 fusion.9.self_ref
  47.3 0.4 copy-done.5
  47.6 0.0 copy-start.3
  47.6 1.0 fusion.8.neigh_ref
  48.7 0.0 copy-done.3
  48.7 0.3 select_reduce_fusion
  49.0 0.0 collective-permute-done
  49.0 1.4 fusion.13.spread_ref
  50.4 94.5 %all-to-all-done.1 = bf16[256,33,2,128]{3,2,1,0:T(2,128)(2,1)} async-done(((bf16[256,33,2,128]{3,2,1,0:T(2,128)(2,1)}), bf16[256,33,2,128]{3,2,1,0:T(2,128)(2,1)}, u32[]{:S(2)}, u32[]{:S(2)}) %all-to-all-start.1) | async-done | bytes 4325408 | tf_op jit(solution)/shard_map/all_to_all | solution.py:308
  144.9 4.2 %unpack.1.rows_ref.own_ref = bf16[384,1536]{1,0:T(8,128)(2,1)S(1)} custom-call(bf16[16896,128]{1,0:T(8,128)(2,1)} %bitcast.6.rows_ref, s32[16,256]{1,0:T(8,128)S(1)} %get-tuple-element.23.groups_ref, bf16[64,768]{1,0:T(8,128)(2,1)S(1)} %gather_fusion), custom_call_target="tpu_custom_call" | custom-call | tf_op jit(solution)/shard_map/unpack/pallas_call | solution.py:195
  149.2 0.3 collective-permute-start.1
  149.5 1.3 layer_first.1
  150.8 1.5 collective-permute-done.1.rows_ref
  152.3 4.4 %layer_second.1 = (bf16[64,512]{1,0:T(8,128)(2,1)S(1)}, bf16[512,1664]{1,0:T(8,128)(2,1)}) custom-call(bf16[384,1536]{1,0:T(8,128)(2,1)S(1)} %collective-permute-done.1.rows_ref, bf16[768,512]{1,0:T(8,128)(2,1)S(1)} %fusion.9.self_ref, bf16[768,512]{1,0:T(8,128)(2,1)S(1)} %fusion.8.neigh_ref, f32[1,512]{1,0:T(1,128)S(1)} %bitcast.28, ...), custom_call_target="tpu_custom_call" | custom-call | tf_op jit(solution)/shard_map/layer_second/pallas_call | solution.py:267
  156.6 4.8 %all-to-all-start.2 = ((bf16[16,32,1664]{2,1,0:T(8,128)(2,1)}), bf16[16,32,1664]{2,1,0:T(8,128)(2,1)S(1)}, u32[]{:S(2)}, u32[]{:S(2)}) async-start(bf16[16,32,1664]{2,1,0:T(8,128)(2,1)} %bitcast.30), calls=%async_computation.2 | async-start | bytes 3407872 | tf_op jit(solution)/shard_map/all_to_all | solution.py:308
  161.5 0.0 collective-permute-start.2
  161.5 1.2 fusion
  162.7 23.4 %all-to-all-done.2.pieces_ref = bf16[16,32,1664]{2,1,0:T(8,128)(2,1)S(1)} async-done(((bf16[16,32,1664]{2,1,0:T(8,128)(2,1)}), bf16[16,32,1664]{2,1,0:T(8,128)(2,1)S(1)}, u32[]{:S(2)}, u32[]{:S(2)}) %all-to-all-start.2) | async-done | bytes 1703968 | tf_op jit(solution)/shard_map/all_to_all | solution.py:308
  186.1 0.9 sum_pieces.1
  187.0 3.4 %all-to-all-start.3 = ((bf16[8,4,1664]{2,1,0:T(4,128)(2,1)}), bf16[8,4,1664]{2,1,0:T(4,128)(2,1)S(1)}, u32[]{:S(2)}, u32[]{:S(2)}) async-start(bf16[8,4,1664]{2,1,0:T(4,128)(2,1)} %sum_pieces.1), calls=%async_computation.3 | async-start | bytes 212992 | tf_op jit(solution)/shard_map/all_to_all | solution.py:308
  190.4 0.0 collective-permute-done.2
  190.4 2.1 %fusion.11 = bf16[64,1024]{1,0:T(8,128)(2,1)} fusion(f32[64,1024]{1,0:T(8,128)} %fusion, bf16[64,512]{1,0:T(8,128)(2,1)S(1)} %collective-permute-done.2, s32[512]{0:T(512)S(1)} %bitcast.39), kind=kOutput, calls=%fused_computation.15 | convolution fusion | flops 67764224 | bytes 460800 | tf_op jit(solution)/shard_map/dot_general | solution.py:29
  192.5 6.6 %all-to-all-done.3 = bf16[8,4,1664]{2,1,0:T(4,128)(2,1)S(1)} async-done(((bf16[8,4,1664]{2,1,0:T(4,128)(2,1)}), bf16[8,4,1664]{2,1,0:T(4,128)(2,1)S(1)}, u32[]{:S(2)}, u32[]{:S(2)}) %all-to-all-start.3) | async-done | bytes 106528 | tf_op jit(solution)/shard_map/all_to_all | solution.py:308
  199.1 0.1 convert_reduce_fusion
  199.2 0.6 slice_bitcast_fusion
  199.8 0.6 slice_reduce_fusion
  (3 shorter events, 0.0 us)
Async XLA Ops:
  0.6 45.6 %copy-start = (bf16[768,1024]{1,0:T(8,128)(2,1)S(1)}, bf16[768,1024]{1,0:T(8,128)(2,1)}, u32[]{:S(2)}) copy-start(bf16[768,1024]{1,0:T(8,128)(2,1)} %param.13) | copy-start | bytes 4718596
  36.0 8.1 %copy-start.2 = (bf16[64,1024]{1,0:T(8,128)(2,1)S(1)}, bf16[64,1024]{1,0:T(8,128)(2,1)}, u32[]{:S(2)}) copy-start(bf16[64,1024]{1,0:T(8,128)(2,1)} %param.16) | copy-start | bytes 393220
  36.0 8.9 %copy-start.6 = (s32[64]{0:T(128)S(1)}, s32[64]{0:T(128)}, u32[]{:S(2)}) copy-start(s32[64]{0:T(128)} %param.10) | copy-start | bytes 772
  36.0 8.9 %copy-start.1 = (bf16[1024,768]{1,0:T(8,128)(2,1)S(1)}, bf16[1024,768]{1,0:T(8,128)(2,1)}, u32[]{:S(2)}) copy-start(bf16[1024,768]{1,0:T(8,128)(2,1)} %features_hbm.1) | copy-start | bytes 4718596
  36.1 9.6 %copy-start.4 = (s32[2,512]{1,0:T(2,128)S(1)}, s32[2,512]{1,0:T(2,128)}, u32[]{:S(2)}) copy-start(s32[2,512]{1,0:T(2,128)} %constant.26.clone) | copy-start | bytes 12292
  36.1 108.9 %all-to-all-start.1 = ((bf16[256,33,2,128]{3,2,1,0:T(2,128)(2,1)}), bf16[256,33,2,128]{3,2,1,0:T(2,128)(2,1)}, u32[]{:S(2)}, u32[]{:S(2)}) async-start(bf16[256,33,2,128]{3,2,1,0:T(2,128)(2,1)} %bitcast.29), calls=%async_computation.1 | async-start | bytes 8650752 | tf_op jit(solution)/shard_map/all_to_all | solution.py:308
  44.8 4.2 %collective-permute-start = (bf16[64,1024]{1,0:T(8,128)(2,1)}, bf16[64,1024]{1,0:T(8,128)(2,1)}, u32[]{:S(2)}, u32[]{:S(2)}) collective-permute-start(bf16[64,1024]{1,0:T(8,128)(2,1)} %multiply_convert_fusion), channel_id=1, source_target_pairs={{0,1},{1,0},{2,3},{3,2},{4,5},{5,4},{6,7},{7,6},{8,9},{9,8},{10,11... | collective-permute-start | bytes 393224 | tf_op jit(solution)/shard_map/ppermute | solution.py:312
  46.2 1.4 copy-start.5
  47.6 1.0 copy-start.3
  149.2 3.1 %collective-permute-start.1 = (bf16[384,1536]{1,0:T(8,128)(2,1)S(1)}, bf16[384,1536]{1,0:T(8,128)(2,1)S(1)}, u32[]{:S(2)}, u32[]{:S(2)}) collective-permute-start(bf16[384,1536]{1,0:T(8,128)(2,1)S(1)} %unpack.1.rows_ref.own_ref), channel_id=1, source_target_pairs={{0,1},{1,0},{2,3},{3,2},{4,5},{5,4},{6,7},{7,6},{8,9},{9,8},{10,11... | collective-permute-start | bytes 3538952 | tf_op jit(solution)/shard_map/ppermute | solution.py:312
  156.6 29.5 %all-to-all-start.2 = ((bf16[16,32,1664]{2,1,0:T(8,128)(2,1)}), bf16[16,32,1664]{2,1,0:T(8,128)(2,1)S(1)}, u32[]{:S(2)}, u32[]{:S(2)}) async-start(bf16[16,32,1664]{2,1,0:T(8,128)(2,1)} %bitcast.30), calls=%async_computation.2 | async-start | bytes 3407872 | tf_op jit(solution)/shard_map/all_to_all | solution.py:308
  161.5 28.9 %collective-permute-start.2 = (bf16[64,512]{1,0:T(8,128)(2,1)S(1)}, bf16[64,512]{1,0:T(8,128)(2,1)S(1)}, u32[]{:S(2)}, u32[]{:S(2)}) collective-permute-start(bf16[64,512]{1,0:T(8,128)(2,1)S(1)} %get-tuple-element.32), channel_id=1, source_target_pairs={{0,1},{1,0},{2,3},{3,2},{4,5},{5,4},{6,7},{7,6},{8,9},{9,8},{10,11... | collective-permute-start | bytes 196616 | tf_op jit(solution)/shard_map/ppermute | solution.py:312
  187.0 12.1 %all-to-all-start.3 = ((bf16[8,4,1664]{2,1,0:T(4,128)(2,1)}), bf16[8,4,1664]{2,1,0:T(4,128)(2,1)S(1)}, u32[]{:S(2)}, u32[]{:S(2)}) async-start(bf16[8,4,1664]{2,1,0:T(4,128)(2,1)} %sum_pieces.1), calls=%async_computation.3 | async-start | bytes 212992 | tf_op jit(solution)/shard_map/all_to_all | solution.py:308

commit v5 on v4

--- a/solution.py
+++ b/solution.py
@@ -15,6 +15,10 @@
 SLOTS = 16
 USED = FAR_CAP + NEAR_CAP
 LANES = 128
+CHUNKS = 4
+HALVES = 2
+PARTS = 4
+SERVED = 4
 PLAN_BLOCK = 256
 BF16 = jnp.bfloat16
 F32 = jnp.float32
@@ -108,109 +112,107 @@
     )(*inputs)
 
 
-def serve_kernel(asked_ref, features_ref, out_ref, spread_out):
-    peers = asked_ref.shape[0]
+def serve_kernel(asked_ref, features_ref, out_hbm, spread_out, out_ref, left):
     rows_dev, width = features_ref.shape
     pieces = width // LANES
     stride = USED * pieces
-    asked = asked_ref[...].astype(F32)
-    lane = lax.broadcasted_iota(jnp.int32, asked.shape, 1)
+    peers = asked_ref.shape[0] // SERVED
+    lane = lax.broadcasted_iota(jnp.int32, (peers, SLOTS), 1)
     row_at = lax.broadcasted_iota(jnp.int32, (peers, rows_dev), 1).astype(F32)
-    picks = []
-    for slot in range(USED):
-        chosen = jnp.sum(jnp.where(lane == slot, asked, 0.0), axis=1, keepdims=True)
-        picks.append((row_at == chosen).astype(F32).astype(BF16))
-    found = dot(jnp.concatenate(picks, axis=0), features_ref[...])
-    for slot in range(USED):
-        rows = found[slot * peers : (slot + 1) * peers]
-        for piece in range(pieces):
-            spread_out[pl.ds(slot * pieces + piece, peers, stride=stride), :] = rows[:, piece * LANES : (piece + 1) * LANES]
-    out_ref[...] = spread_out[...].astype(BF16)
-
-
-def serve(asked, features, steps=4):
+    copies = []
+    for part in range(SERVED):
+        asked = asked_ref[part * peers : (part + 1) * peers].astype(F32)
+        picks = []
+        for slot in range(USED):
+            chosen = jnp.sum(jnp.where(lane == slot, asked, 0.0), axis=1, keepdims=True)
+            picks.append((row_at == chosen).astype(F32).astype(BF16))
+        found = dot(jnp.concatenate(picks, axis=0), features_ref[...])
+        first = part * peers * stride
+        for slot in range(USED):
+            rows = found[slot * peers : (slot + 1) * peers]
+            for piece in range(pieces):
+                at = first + slot * pieces + piece
+                spread_out[pl.ds(at, peers, stride=stride), :] = rows[:, piece * LANES : (piece + 1) * LANES]
+        here = pl.ds(first, peers * stride)
+        out_ref[here, :] = spread_out[here, :].astype(BF16)
+        copies.append(pltpu.make_async_copy(out_ref.at[here], out_hbm.at[here], left.at[part]))
+        copies[-1].start()
+    for copy in copies:
+        copy.wait()
+
+
+def serve(asked, features):
     devices = asked.shape[0]
-    rows_dev, width = features.shape
-    peers = devices // steps
-    rows = USED * width // LANES
+    shape = (devices * USED * features.shape[1] // LANES, LANES)
     return pl.pallas_call(
         serve_kernel,
-        grid=(steps,),
-        in_specs=[
-            pl.BlockSpec((peers, SLOTS), lambda i: (i, 0)),
-            ON_CHIP,
-        ],
-        out_specs=pl.BlockSpec((peers * rows, LANES), lambda i: (i, 0)),
-        out_shape=pltpu.HBM((devices * rows, LANES), BF16),
-        scratch_shapes=[pltpu.VMEM((peers * rows, LANES), F32)],
+        in_specs=[ON_CHIP, ON_CHIP],
+        out_specs=pl.BlockSpec(memory_space=pltpu.HBM),
+        out_shape=pltpu.HBM(shape, BF16),
+        scratch_shapes=[pltpu.VMEM(shape, F32), pltpu.VMEM(shape, BF16), pltpu.SemaphoreType.DMA((SERVED,))],
         compiler_params=pltpu.CompilerParams(vmem_limit_bytes=KERNEL_VMEM),
         name="serve",
         interpret=INTERPRET,
-    )(asked, on_chip(features))
-
-
-def unpack_kernel(steps, fan_one, fan_two, rows_ref, groups_ref, seed_ref, out_ref, wide, far_acc, near_acc):
-    step = pl.program_id(0)
+    )(on_chip(asked), on_chip(features))
+
+
+def unpack_kernel(fan_one, fan_two, rows_hbm, groups_ref, seed_ref, out_ref, rows_ref, wide, far_acc, near_acc, arrived):
     seeds, width = seed_ref.shape
     pieces = width // LANES
     stride = USED * pieces
     near_total = near_acc.shape[0]
     peers = groups_ref.shape[1]
-
-    @pl.when(step == 0)
-    def _():
-        far_acc[...] = jnp.zeros_like(far_acc)
-        near_acc[...] = jnp.zeros_like(near_acc)
-
-    wide[...] = rows_ref[...].astype(F32)
-    group_at = lax.broadcasted_iota(jnp.int32, (near_total, peers), 0)
-
-    def taken(slots):
-        rows, picks = [], []
-        for slot in slots:
-            at = [wide[pl.ds(slot * pieces + piece, peers, stride=stride), :] for piece in range(pieces)]
-            rows.append(jnp.concatenate(at, axis=1).astype(BF16))
-            picks.append((group_at == groups_ref[slot : slot + 1, :]).astype(F32).astype(BF16))
-        return dot(jnp.concatenate(picks, axis=1), jnp.concatenate(rows, axis=0))
-
-    far_acc[...] += taken(range(FAR_CAP))
-    near_acc[...] += taken(range(FAR_CAP, USED))
-
-    @pl.when(step == steps - 1)
-    def _():
-        out_ref[:near_total, :width] = near_acc[...].astype(BF16)
-        out_ref[near_total:, :width] = seed_ref[...]
-        out_ref[:near_total, width:] = (far_acc[...] / fan_two).astype(BF16)
-        summed = near_acc[:seeds]
-        for k in range(1, fan_one):
-            summed = summed + near_acc[k * seeds : (k + 1) * seeds]
-        out_ref[near_total:, width:] = (summed / fan_one).astype(BF16)
-
-
-def unpack(rows, groups, seed_x, fan_one, fan_two, steps=2):
-    total = rows.shape[0]
+    share = rows_ref.shape[0] // CHUNKS
+    chunks = [pl.ds(at * share, share) for at in range(CHUNKS)]
+    copies = [
+        pltpu.make_async_copy(rows_hbm.at[here], rows_ref.at[here], arrived.at[at]) for at, here in enumerate(chunks)
+    ]
+    for copy in copies:
+        copy.start()
+    half = peers // HALVES
+    group_at = lax.broadcasted_iota(jnp.int32, (near_total, half), 0)
+    for part in range(HALVES):
+        for at in range(part * CHUNKS // HALVES, (part + 1) * CHUNKS // HALVES):
+            copies[at].wait()
+            wide[chunks[at], :] = rows_ref[chunks[at], :].astype(F32)
+        for slots, acc in ((range(FAR_CAP), far_acc), (range(FAR_CAP, USED), near_acc)):
+            picks, rows = [], []
+            for slot in slots:
+                groups = groups_ref[slot : slot + 1, part * half : (part + 1) * half]
+                picks.append((group_at == groups).astype(F32).astype(BF16))
+                first = part * half * stride + slot * pieces
+                at = [wide[pl.ds(first + piece, half, stride=stride), :] for piece in range(pieces)]
+                rows.append(jnp.concatenate(at, axis=1).astype(BF16))
+            taken = dot(jnp.concatenate(picks, axis=1), jnp.concatenate(rows, axis=0))
+            acc[...] = taken if part == 0 else acc[...] + taken
+    out_ref[:near_total, :width] = near_acc[...].astype(BF16)
+    out_ref[near_total:, :width] = seed_ref[...]
+    out_ref[:near_total, width:] = (far_acc[...] / fan_two).astype(BF16)
+    summed = near_acc[:seeds]
+    for k in range(1, fan_one):
+        summed = summed + near_acc[k * seeds : (k + 1) * seeds]
+    out_ref[near_total:, width:] = (summed / fan_one).astype(BF16)
+
+
+def unpack(rows, groups, seed_x, fan_one, fan_two):
     seeds, width = seed_x.shape
-    peers = groups.shape[1] // steps
     near_total = seeds * fan_one
     return pl.pallas_call(
-        functools.partial(unpack_kernel, steps, fan_one, fan_two),
-        grid=(steps,),
-        in_specs=[
-            pl.BlockSpec((total // steps, LANES), lambda i: (i, 0)),
-            pl.BlockSpec((groups.shape[0], peers), lambda i: (0, i)),
-            pl.BlockSpec((seeds, width), lambda i: (0, 0)),
-        ],
+        functools.partial(unpack_kernel, fan_one, fan_two),
+        in_specs=[pl.BlockSpec(memory_space=pltpu.HBM), ON_CHIP, ON_CHIP],
         out_specs=ON_CHIP,
         out_shape=pltpu.VMEM((near_total + seeds, 2 * width), BF16),
         scratch_shapes=[
-            pltpu.VMEM((total // steps, LANES), F32),
+            pltpu.VMEM(rows.shape, BF16),
+            pltpu.VMEM(rows.shape, F32),
             pltpu.VMEM((near_total, width), F32),
             pltpu.VMEM((near_total, width), F32),
+            pltpu.SemaphoreType.DMA((CHUNKS,)),
         ],
         compiler_params=pltpu.CompilerParams(vmem_limit_bytes=KERNEL_VMEM),
         name="unpack",
         interpret=INTERPRET,
-    )(rows, groups, seed_x)
+    )(pltpu.with_memory_space_constraint(rows, pltpu.HBM), on_chip(groups), on_chip(seed_x))
 
 
 def forward(fan_one, rows_ref, self_ref, neigh_ref, bias_ref, spread_ref, embedded_ref):
@@ -227,61 +229,56 @@
     return jnp.where(pre > 0, jnp.concatenate([spread] * (1 + fan_one), axis=0), 0.0).T
 
 
-def first_kernel(fan_one, part, rows_ref, self_ref, neigh_ref, bias_ref, spread_ref, embedded_ref, turned_ref):
-    here = pl.ds(pl.multiple_of(pl.program_id(0) * part, part), part)
+def first_kernel(fan_one, rows_ref, self_ref, neigh_ref, bias_ref, spread_ref, embedded_ref, turned_ref):
     turned = forward(fan_one, rows_ref, self_ref, neigh_ref, bias_ref, spread_ref, embedded_ref)
-    turned_ref[here, :] = turned.astype(BF16)
+    turned_ref[...] = turned.astype(BF16)
 
 
 def second_kernel(
-    fan_one, part, rows_ref, self_ref, neigh_ref, bias_ref, spread_ref, own_ref, turned_ref, embedded_ref, grad_ref, both
+    fan_one, rows_ref, self_ref, neigh_ref, bias_ref, spread_ref, own_ref, own_turned_ref, embedded_ref, grad_hbm,
+    both, turned, grad_ref, left,
 ):
     count, columns = own_ref.shape
-    here = pl.ds(pl.multiple_of(pl.program_id(0) * part, part), part)
-
-    @pl.when(pl.program_id(0) == 0)
-    def _():
-        both[:count] = own_ref[...]
-        both[count:] = rows_ref[...]
-
+    both[:count] = own_ref[...]
+    both[count:] = rows_ref[...]
+    turned[:, :count] = own_turned_ref[...]
     pair = forward(fan_one, rows_ref, self_ref, neigh_ref, bias_ref, spread_ref, embedded_ref)
-    turned = jnp.concatenate([turned_ref[here, :], pair.astype(BF16)], axis=1)
-    grad_ref[:, :columns] = dot(turned, both[...]).astype(BF16)
-    summed = jnp.sum(turned.astype(F32), axis=1, keepdims=True)
-    grad_ref[:, columns:] = jnp.broadcast_to(summed, (part, LANES)).astype(BF16)
-
-
-def layer(rows, w_self, w_neigh, bias, spread, fan_one, own=(), steps=2):
+    turned[:, count:] = pair.astype(BF16)
+    part = turned.shape[0] // PARTS
+    copies = []
+    for at in range(PARTS):
+        here = pl.ds(at * part, part)
+        grad_ref[here, :columns] = dot(turned[here, :], both[...]).astype(BF16)
+        summed = jnp.sum(turned[here, :].astype(F32), axis=1, keepdims=True)
+        grad_ref[here, columns:] = jnp.broadcast_to(summed, (part, LANES)).astype(BF16)
+        copies.append(pltpu.make_async_copy(grad_ref.at[here], grad_hbm.at[here], left.at[at]))
+        copies[-1].start()
+    for copy in copies:
+        copy.wait()
+
+
+def layer(rows, w_self, w_neigh, bias, spread, fan_one, own=()):
     count, both = rows.shape
-    width, hidden = w_self.shape
-    part = hidden // steps
+    hidden = w_self.shape[1]
     seeds = spread.shape[0]
-    weights = pl.BlockSpec((width, part), lambda i: (0, i))
-    half = pl.BlockSpec((seeds, part), lambda i: (0, i))
-    if own:
-        last_spec = pl.BlockSpec((part, both + LANES), lambda i: (i, 0))
-        last_shape = pltpu.HBM((hidden, both + LANES), BF16)
-    else:
-        last_spec = ON_CHIP
-        last_shape = pltpu.VMEM((hidden, count), BF16)
-    return pl.pallas_call(
-        functools.partial(second_kernel if own else first_kernel, fan_one, part),
-        grid=(steps,),
-        in_specs=[
-            ON_CHIP,
-            weights,
-            weights,
-            pl.BlockSpec((1, part), lambda i: (0, i)),
-            half,
-            *[ON_CHIP for _ in own],
-        ],
-        out_specs=(half, last_spec),
-        out_shape=(jax.ShapeDtypeStruct((seeds, hidden), BF16), last_shape),
-        scratch_shapes=[pltpu.VMEM((2 * count, both), BF16)] if own else [],
+    inputs = (rows, w_self, w_neigh, bias, spread, *own)
+    grads = (hidden, both + LANES)
+    scratch = [
+        pltpu.VMEM((2 * count, both), BF16),
+        pltpu.VMEM((hidden, 2 * count), BF16),
+        pltpu.VMEM(grads, BF16),
+        pltpu.SemaphoreType.DMA((PARTS,)),
+    ]
+    return pl.pallas_call(
+        functools.partial(second_kernel if own else first_kernel, fan_one),
+        in_specs=[ON_CHIP] * len(inputs),
+        out_specs=(ON_CHIP, pl.BlockSpec(memory_space=pltpu.HBM) if own else ON_CHIP),
+        out_shape=(pltpu.VMEM((seeds, hidden), BF16), pltpu.HBM(grads, BF16) if own else pltpu.VMEM((hidden, count), BF16)),
+        scratch_shapes=scratch if own else [],
         compiler_params=pltpu.CompilerParams(vmem_limit_bytes=KERNEL_VMEM),
         name="layer_second" if own else "layer_first",
         interpret=INTERPRET,
-    )(on_chip(rows), w_self, w_neigh, bias, spread, *[on_chip(x) for x in own])
+    )(*[on_chip(x) for x in inputs])
 
 
 def sum_kernel(pieces_ref, out_ref):

time: 201 us -> 198 us (0.985)
  Pallas kernels: 19.8 us -> 17 us
  transfers between devices with their start and end apart: 6 -> 6, of which waited for: 4 -> 4; matrix products, arithmetic and copies ran while one was open for 4% -> 5% of each run, Pallas kernels for 1% -> 1%
where the time goes in v5:
time: 198 us
  waiting for transfers between devices  126 us (64%)
  blocking collectives  26.4 us (13%)
  Pallas kernels  17 us (9%)
  starting transfers between devices  16.5 us (8%)
  matrix products  7.26 us (4%)
  local copies, waits for them, and re-layouts  2.36 us (1%)
    all_to_all x3, waiting for transfers between devices, exchange(): return lax.all_to_all(pieces, axes, split_axis=0, concat_axis=0, tiled=True)  124 us
    all_to_all x1, blocking collectives, exchange(): return lax.all_to_all(pieces, axes, split_axis=0, concat_axis=0, tiled=True)  26.4 us
    all_to_all x3, starting transfers between devices, exchange(): return lax.all_to_all(pieces, axes, split_axis=0, concat_axis=0, tiled=True)  16.3 us
    dot_general x6, matrix products, dot(): return lax.dot_general(left, right, dims, preferred_element_type=F32)  7.26 us
    pallas_call x1, Pallas kernels, serve(): pl.pallas_call(serve_kernel, in_specs=[ON_CHIP, ON_CHIP], out_specs=pl.Bl...  6.22 us
    pallas_call x2, Pallas kernels, layer(): pl.pallas_call(functools.partial(second_kernel if own else first_kernel,...  3.98 us
  transfers between devices with their start and end apart: 6, of which 4 were waited for; matrix products, arithmetic and copies ran while one was open for 5% of the time, Pallas kernels for 1%

profile of v5, /device:TPU:8, one launch (start us, length us, event | category | flops | bytes accessed | tf_op | source)
XLA Modules:
  0.0 197.9 jit_solution(1565197285283837834)
XLA Ops:
  0.6 0.0 copy-start
  0.6 2.1 %plan.1 = (s32[256,16]{1,0:T(8,128)S(1)}, s32[16,256]{1,0:T(8,128)S(1)}, bf16[1024,768]{1,0:T(8,128)(2,1)S(1)}) custom-call(s32[5,5,64]{2,1,0:T(8,128)} %bitcast.31, s32[5,64]{1,0:T(8,128)} %bitcast.38, bf16[1024,768]{1,0:T(8,128)(2,1)} %features_hbm.1), custom_call_target="tpu_custom_call" | custom-call | tf_op jit(solution)/shard_map/plan/pallas_call | solution.py:99
  2.7 26.4 %all_to_all.20 = s32[256,1,16]{2,1,0:T(1,128)S(1)} all-to-all(s32[256,1,16]{2,1,0:T(1,128)S(1)} %bitcast.26), channel_id=1, replica_groups=mesh['gx'=4,'gy_0'=8,'gy_1'=4,'gy_2'=2] {'gx','gy_0','gy_1','gy_2'}, dimensions={0} | all-to-all | bytes 32768 | tf_op jit(solution)/shard_map/all_to_all | solution.py:305
  29.1 6.2 %serve.1 = bf16[16896,128]{1,0:T(8,128)(2,1)} custom-call(s32[256,16]{1,0:T(8,128)S(1)} %bitcast.25, bf16[1024,768]{1,0:T(8,128)(2,1)S(1)} %get-tuple-element.20.features_ref), custom_call_target="tpu_custom_call" | custom-call | tf_op jit(solution)/shard_map/serve/pallas_call | solution.py:147
  35.4 0.0 copy-start.2
  35.4 0.0 copy-start.6
  35.4 0.0 copy-start.1
  35.4 0.0 copy-start.4
  35.4 8.1 %all-to-all-start.1 = ((bf16[256,33,2,128]{3,2,1,0:T(2,128)(2,1)}), bf16[256,33,2,128]{3,2,1,0:T(2,128)(2,1)}, u32[]{:S(2)}, u32[]{:S(2)}) async-start(bf16[256,33,2,128]{3,2,1,0:T(2,128)(2,1)} %bitcast.29), calls=%async_computation.1 | async-start | bytes 8650752 | tf_op jit(solution)/shard_map/all_to_all | solution.py:305
  43.5 0.0 copy-done.2
  43.5 0.7 multiply_convert_fusion
  44.2 0.1 collective-permute-start
  44.3 0.0 copy-done.6
  44.3 0.0 copy-done.1
  44.4 0.7 gather_fusion
  45.1 0.0 copy-done.4
  45.1 0.5 fusion.12.spread_ref
  45.6 0.0 copy-done
  45.6 0.0 copy-start.5
  45.6 1.0 fusion.9.self_ref
  46.7 0.4 copy-done.5
  47.0 0.0 copy-start.3
  47.0 1.0 fusion.8.neigh_ref
  48.0 0.0 copy-done.3
  48.1 0.3 select_reduce_fusion
  48.4 0.0 collective-permute-done
  48.4 1.4 fusion.13.spread_ref
  49.8 94.5 %all-to-all-done.1 = bf16[256,33,2,128]{3,2,1,0:T(2,128)(2,1)} async-done(((bf16[256,33,2,128]{3,2,1,0:T(2,128)(2,1)}), bf16[256,33,2,128]{3,2,1,0:T(2,128)(2,1)}, u32[]{:S(2)}, u32[]{:S(2)}) %all-to-all-start.1) | async-done | bytes 4325408 | tf_op jit(solution)/shard_map/all_to_all | solution.py:305
  144.3 3.8 %unpack.1.rows_ref.own_ref = bf16[384,1536]{1,0:T(8,128)(2,1)S(1)} custom-call(bf16[16896,128]{1,0:T(8,128)(2,1)} %bitcast.6.rows_hbm, s32[16,256]{1,0:T(8,128)S(1)} %get-tuple-element.23.groups_ref, bf16[64,768]{1,0:T(8,128)(2,1)S(1)} %gather_fusion), custom_call_target="tpu_custom_call" | custom-call | tf_op jit(solution)/shard_map/unpack/pallas_call | solution.py:200
  148.1 0.1 collective-permute-start.1
  148.2 0.9 layer_first.1
  149.2 1.9 collective-permute-done.1.rows_ref
  151.1 3.0 %layer_second.1 = (bf16[64,512]{1,0:T(8,128)(2,1)S(1)}, bf16[512,1664]{1,0:T(8,128)(2,1)}) custom-call(bf16[384,1536]{1,0:T(8,128)(2,1)S(1)} %collective-permute-done.1.rows_ref, bf16[768,512]{1,0:T(8,128)(2,1)S(1)} %fusion.9.self_ref, bf16[768,512]{1,0:T(8,128)(2,1)S(1)} %fusion.8.neigh_ref, f32[1,512]{1,0:T(1,128)S(1)} %bitcast.28, ...), custom_call_target="tpu_custom_call" | custom-call | tf_op jit(solution)/shard_map/layer_second/pallas_call | solution.py:272
  154.1 4.8 %all-to-all-start.2 = ((bf16[16,32,1664]{2,1,0:T(8,128)(2,1)}), bf16[16,32,1664]{2,1,0:T(8,128)(2,1)S(1)}, u32[]{:S(2)}, u32[]{:S(2)}) async-start(bf16[16,32,1664]{2,1,0:T(8,128)(2,1)} %bitcast.30), calls=%async_computation.2 | async-start | bytes 3407872 | tf_op jit(solution)/shard_map/all_to_all | solution.py:305
  159.0 0.0 collective-permute-start.2
  159.0 1.2 fusion
  160.2 23.4 %all-to-all-done.2.pieces_ref = bf16[16,32,1664]{2,1,0:T(8,128)(2,1)S(1)} async-done(((bf16[16,32,1664]{2,1,0:T(8,128)(2,1)}), bf16[16,32,1664]{2,1,0:T(8,128)(2,1)S(1)}, u32[]{:S(2)}, u32[]{:S(2)}) %all-to-all-start.2) | async-done | bytes 1703968 | tf_op jit(solution)/shard_map/all_to_all | solution.py:305
  183.6 0.9 sum_pieces.1
  184.5 3.4 %all-to-all-start.3 = ((bf16[8,4,1664]{2,1,0:T(4,128)(2,1)}), bf16[8,4,1664]{2,1,0:T(4,128)(2,1)S(1)}, u32[]{:S(2)}, u32[]{:S(2)}) async-start(bf16[8,4,1664]{2,1,0:T(4,128)(2,1)} %sum_pieces.1), calls=%async_computation.3 | async-start | bytes 212992 | tf_op jit(solution)/shard_map/all_to_all | solution.py:305
  187.8 0.0 collective-permute-done.2
  187.8 2.1 %fusion.11 = bf16[64,1024]{1,0:T(8,128)(2,1)} fusion(f32[64,1024]{1,0:T(8,128)} %fusion, bf16[64,512]{1,0:T(8,128)(2,1)S(1)} %collective-permute-done.2, s32[512]{0:T(512)S(1)} %bitcast.39), kind=kOutput, calls=%fused_computation.15 | convolution fusion | flops 67764224 | bytes 460800 | tf_op jit(solution)/shard_map/dot_general | solution.py:33
  190.0 6.6 %all-to-all-done.3 = bf16[8,4,1664]{2,1,0:T(4,128)(2,1)S(1)} async-done(((bf16[8,4,1664]{2,1,0:T(4,128)(2,1)}), bf16[8,4,1664]{2,1,0:T(4,128)(2,1)S(1)}, u32[]{:S(2)}, u32[]{:S(2)}) %all-to-all-start.3) | async-done | bytes 106528 | tf_op jit(solution)/shard_map/all_to_all | solution.py:305
  196.6 0.1 convert_reduce_fusion
  196.6 0.6 slice_bitcast_fusion
  197.2 0.6 slice_reduce_fusion
  (3 shorter events, 0.0 us)
Async XLA Ops:
  0.6 45.0 %copy-start = (bf16[768,1024]{1,0:T(8,128)(2,1)S(1)}, bf16[768,1024]{1,0:T(8,128)(2,1)}, u32[]{:S(2)}) copy-start(bf16[768,1024]{1,0:T(8,128)(2,1)} %param.13) | copy-start | bytes 4718596
  35.4 8.1 %copy-start.2 = (bf16[64,1024]{1,0:T(8,128)(2,1)S(1)}, bf16[64,1024]{1,0:T(8,128)(2,1)}, u32[]{:S(2)}) copy-start(bf16[64,1024]{1,0:T(8,128)(2,1)} %param.16) | copy-start | bytes 393220
  35.4 8.9 %copy-start.6 = (s32[64]{0:T(128)S(1)}, s32[64]{0:T(128)}, u32[]{:S(2)}) copy-start(s32[64]{0:T(128)} %param.10) | copy-start | bytes 772
  35.4 9.0 %copy-start.1 = (bf16[1024,768]{1,0:T(8,128)(2,1)S(1)}, bf16[1024,768]{1,0:T(8,128)(2,1)}, u32[]{:S(2)}) copy-start(bf16[1024,768]{1,0:T(8,128)(2,1)} %features_hbm.1) | copy-start | bytes 4718596
  35.4 9.7 %copy-start.4 = (s32[2,512]{1,0:T(2,128)S(1)}, s32[2,512]{1,0:T(2,128)}, u32[]{:S(2)}) copy-start(s32[2,512]{1,0:T(2,128)} %constant.26.clone) | copy-start | bytes 12292
  35.4 108.9 %all-to-all-start.1 = ((bf16[256,33,2,128]{3,2,1,0:T(2,128)(2,1)}), bf16[256,33,2,128]{3,2,1,0:T(2,128)(2,1)}, u32[]{:S(2)}, u32[]{:S(2)}) async-start(bf16[256,33,2,128]{3,2,1,0:T(2,128)(2,1)} %bitcast.29), calls=%async_computation.1 | async-start | bytes 8650752 | tf_op jit(solution)/shard_map/all_to_all | solution.py:305
  44.2 4.2 %collective-permute-start = (bf16[64,1024]{1,0:T(8,128)(2,1)}, bf16[64,1024]{1,0:T(8,128)(2,1)}, u32[]{:S(2)}, u32[]{:S(2)}) collective-permute-start(bf16[64,1024]{1,0:T(8,128)(2,1)} %multiply_convert_fusion), channel_id=1, source_target_pairs={{0,1},{1,0},{2,3},{3,2},{4,5},{5,4},{6,7},{7,6},{8,9},{9,8},{10,11... | collective-permute-start | bytes 393224 | tf_op jit(solution)/shard_map/ppermute | solution.py:309
  45.6 1.4 copy-start.5
  47.0 1.0 copy-start.3
  148.1 2.9 %collective-permute-start.1 = (bf16[384,1536]{1,0:T(8,128)(2,1)S(1)}, bf16[384,1536]{1,0:T(8,128)(2,1)S(1)}, u32[]{:S(2)}, u32[]{:S(2)}) collective-permute-start(bf16[384,1536]{1,0:T(8,128)(2,1)S(1)} %unpack.1.rows_ref.own_ref), channel_id=1, source_target_pairs={{0,1},{1,0},{2,3},{3,2},{4,5},{5,4},{6,7},{7,6},{8,9},{9,8},{10,11... | collective-permute-start | bytes 3538952 | tf_op jit(solution)/shard_map/ppermute | solution.py:309
  154.1 29.5 %all-to-all-start.2 = ((bf16[16,32,1664]{2,1,0:T(8,128)(2,1)}), bf16[16,32,1664]{2,1,0:T(8,128)(2,1)S(1)}, u32[]{:S(2)}, u32[]{:S(2)}) async-start(bf16[16,32,1664]{2,1,0:T(8,128)(2,1)} %bitcast.30), calls=%async_computation.2 | async-start | bytes 3407872 | tf_op jit(solution)/shard_map/all_to_all | solution.py:305
  159.0 28.9 %collective-permute-start.2 = (bf16[64,512]{1,0:T(8,128)(2,1)S(1)}, bf16[64,512]{1,0:T(8,128)(2,1)S(1)}, u32[]{:S(2)}, u32[]{:S(2)}) collective-permute-start(bf16[64,512]{1,0:T(8,128)(2,1)S(1)} %get-tuple-element.32), channel_id=1, source_target_pairs={{0,1},{1,0},{2,3},{3,2},{4,5},{5,4},{6,7},{7,6},{8,9},{9,8},{10,11... | collective-permute-start | bytes 196616 | tf_op jit(solution)/shard_map/ppermute | solution.py:309
  184.5 12.1 %all-to-all-start.3 = ((bf16[8,4,1664]{2,1,0:T(4,128)(2,1)}), bf16[8,4,1664]{2,1,0:T(4,128)(2,1)S(1)}, u32[]{:S(2)}, u32[]{:S(2)}) async-start(bf16[8,4,1664]{2,1,0:T(4,128)(2,1)} %sum_pieces.1), calls=%async_computation.3 | async-start | bytes 212992 | tf_op jit(solution)/shard_map/all_to_all | solution.py:305

commit v6 on v5

--- a/solution.py
+++ b/solution.py
@@ -18,7 +18,7 @@
 CHUNKS = 4
 HALVES = 2
 PARTS = 4
-SERVED = 4
+SERVED = 8
 PLAN_BLOCK = 256
 BF16 = jnp.bfloat16
 F32 = jnp.float32
@@ -301,6 +301,40 @@
     )(on_chip(pieces))
 
 
+def last_kernel(pieces_ref, self_hbm, neigh_hbm, bias_hbm, self_ref, neigh_ref, bias_ref, left):
+    share, width = self_ref.shape
+    summed = pieces_ref[0].astype(F32)
+    for at in range(1, pieces_ref.shape[0]):
+        summed = summed + pieces_ref[at].astype(F32)
+    self_ref[...] = summed[:, :width]
+    neigh_ref[...] = summed[:, width : 2 * width]
+    square = (share, share)
+    here = lax.broadcasted_iota(jnp.int32, square, 0) == lax.broadcasted_iota(jnp.int32, square, 1)
+    column = jnp.broadcast_to(summed[:, 2 * width : 2 * width + 1], square)
+    bias_ref[...] = jnp.sum(jnp.where(here, column, 0.0), axis=0, keepdims=True)
+    pairs = ((self_ref, self_hbm), (neigh_ref, neigh_hbm), (bias_ref, bias_hbm))
+    copies = [pltpu.make_async_copy(*pair, left.at[at]) for at, pair in enumerate(pairs)]
+    for copy in copies:
+        copy.start()
+    for copy in copies:
+        copy.wait()
+
+
+def last(pieces, width):
+    share = pieces.shape[1]
+    shapes = ((share, width), (share, width), (1, share))
+    return pl.pallas_call(
+        last_kernel,
+        in_specs=[ON_CHIP],
+        out_specs=(pl.BlockSpec(memory_space=pltpu.HBM),) * 3,
+        out_shape=tuple(pltpu.HBM(shape, F32) for shape in shapes),
+        scratch_shapes=[*[pltpu.VMEM(shape, F32) for shape in shapes], pltpu.SemaphoreType.DMA((3,))],
+        compiler_params=pltpu.CompilerParams(vmem_limit_bytes=KERNEL_VMEM),
+        name="last",
+        interpret=INTERPRET,
+    )(on_chip(pieces))
+
+
 def exchange(pieces, axes):
     return lax.all_to_all(pieces, axes, split_axis=0, concat_axis=0, tiled=True)
 
@@ -350,8 +384,9 @@
     embedded = (dot(embedded_own, turn, NT) + dot(swapped(embedded_pair), turn_other, NT)).astype(BF16)
 
     pieces = exchange(grad.reshape(split_x * split_y, -1, grad.shape[-1]), ("gx", "gy_1"))
-    grad = exchange(sum_pieces(pieces, split_z), ("gy_0",)).astype(F32).sum(axis=0)
-    return (embedded, grad[:, :width].T, grad[:, width : 2 * width].T, grad[:, 2 * width])
+    pieces = exchange(sum_pieces(pieces, split_z), ("gy_0",))
+    grad_self, grad_neigh, grad_bias = last(pieces, width)
+    return (embedded, grad_self.T, grad_neigh.T, grad_bias.reshape(-1))
 
 
 def solution(mesh):

time: 198 us -> 198 us (level)
  no operation moved by 1% of the time
where the time goes in v6:
time: 198 us; the launch traced here: 197 us
  waiting for transfers between devices  126 us (64%)
  blocking collectives  26.4 us (13%)
  Pallas kernels  17.5 us (9%)
  starting transfers between devices  16.5 us (8%)
  matrix products  7.28 us (4%)
    all_to_all x3, waiting for transfers between devices, exchange(): return lax.all_to_all(pieces, axes, split_axis=0, concat_axis=0, tiled=True)  124 us
    all_to_all x1, blocking collectives, exchange(): return lax.all_to_all(pieces, axes, split_axis=0, concat_axis=0, tiled=True)  26.4 us
    all_to_all x3, starting transfers between devices, exchange(): return lax.all_to_all(pieces, axes, split_axis=0, concat_axis=0, tiled=True)  16.3 us
    dot_general x6, matrix products, dot(): return lax.dot_general(left, right, dims, preferred_element_type=F32)  7.28 us
    pallas_call x1, Pallas kernels, serve(): pl.pallas_call(serve_kernel, in_specs=[ON_CHIP, ON_CHIP], out_specs=pl.Bl...  6.07 us
  transfers between devices with their start and end apart: 6, of which 4 were waited for; matrix products, arithmetic and copies ran while one was open for 5% of the time, Pallas kernels for 1%

profile of v6, /device:TPU:8, one launch (start us, length us, event | category | flops | bytes accessed | tf_op | source)
XLA Modules:
  0.0 197.2 jit_solution(4988755693019256263)
XLA Ops:
  0.6 0.0 copy-start
  0.6 2.1 %plan.1 = (s32[256,16]{1,0:T(8,128)S(1)}, s32[16,256]{1,0:T(8,128)S(1)}, bf16[1024,768]{1,0:T(8,128)(2,1)S(1)}) custom-call(s32[5,5,64]{2,1,0:T(8,128)} %bitcast.30, s32[5,64]{1,0:T(8,128)} %bitcast.37, bf16[1024,768]{1,0:T(8,128)(2,1)} %features_hbm.1), custom_call_target="tpu_custom_call" | custom-call | tf_op jit(solution)/shard_map/plan/pallas_call | solution.py:99
  2.7 26.4 %all_to_all.20 = s32[256,1,16]{2,1,0:T(1,128)S(1)} all-to-all(s32[256,1,16]{2,1,0:T(1,128)S(1)} %bitcast.25), channel_id=1, replica_groups=mesh['gx'=4,'gy_0'=8,'gy_1'=4,'gy_2'=2] {'gx','gy_0','gy_1','gy_2'}, dimensions={0} | all-to-all | bytes 32768 | tf_op jit(solution)/shard_map/all_to_all | solution.py:339
  29.1 6.1 %serve.1 = bf16[16896,128]{1,0:T(8,128)(2,1)} custom-call(s32[256,16]{1,0:T(8,128)S(1)} %bitcast.24, bf16[1024,768]{1,0:T(8,128)(2,1)S(1)} %get-tuple-element.23.features_ref), custom_call_target="tpu_custom_call" | custom-call | tf_op jit(solution)/shard_map/serve/pallas_call | solution.py:147
  35.2 0.0 copy-start.2
  35.2 0.0 copy-start.6
  35.2 0.0 copy-start.1
  35.3 0.0 copy-start.4
  35.3 8.1 %all-to-all-start.1 = ((bf16[256,33,2,128]{3,2,1,0:T(2,128)(2,1)}), bf16[256,33,2,128]{3,2,1,0:T(2,128)(2,1)}, u32[]{:S(2)}, u32[]{:S(2)}) async-start(bf16[256,33,2,128]{3,2,1,0:T(2,128)(2,1)} %bitcast.28), calls=%async_computation.1 | async-start | bytes 8650752 | tf_op jit(solution)/shard_map/all_to_all | solution.py:339
  43.4 0.0 copy-done.2
  43.4 0.7 multiply_convert_fusion
  44.0 0.1 collective-permute-start
  44.2 0.0 copy-done.6
  44.2 0.0 copy-done.1
  44.2 0.7 gather_fusion
  44.9 0.0 copy-done.4
  44.9 0.5 fusion.12.spread_ref
  45.4 0.0 copy-done
  45.4 0.0 copy-start.5
  45.5 1.0 fusion.9.self_ref
  46.5 0.4 copy-done.5
  46.9 0.0 copy-start.3
  46.9 1.0 fusion.8.neigh_ref
  47.9 0.0 copy-done.3
  47.9 0.3 select_reduce_fusion
  48.2 0.0 collective-permute-done
  48.2 1.4 fusion.13.spread_ref
  49.6 94.5 %all-to-all-done.1 = bf16[256,33,2,128]{3,2,1,0:T(2,128)(2,1)} async-done(((bf16[256,33,2,128]{3,2,1,0:T(2,128)(2,1)}), bf16[256,33,2,128]{3,2,1,0:T(2,128)(2,1)}, u32[]{:S(2)}, u32[]{:S(2)}) %all-to-all-start.1) | async-done | bytes 4325408 | tf_op jit(solution)/shard_map/all_to_all | solution.py:339
  144.1 3.8 %unpack.1.rows_ref.own_ref = bf16[384,1536]{1,0:T(8,128)(2,1)S(1)} custom-call(bf16[16896,128]{1,0:T(8,128)(2,1)} %bitcast.6.rows_hbm, s32[16,256]{1,0:T(8,128)S(1)} %get-tuple-element.26.groups_ref, bf16[64,768]{1,0:T(8,128)(2,1)S(1)} %gather_fusion), custom_call_target="tpu_custom_call" | custom-call | tf_op jit(solution)/shard_map/unpack/pallas_call | solution.py:200
  148.0 0.1 collective-permute-start.1
  148.1 0.9 layer_first.1
  149.0 1.9 collective-permute-done.1.rows_ref
  150.9 3.0 %layer_second.1 = (bf16[64,512]{1,0:T(8,128)(2,1)S(1)}, bf16[512,1664]{1,0:T(8,128)(2,1)}) custom-call(bf16[384,1536]{1,0:T(8,128)(2,1)S(1)} %collective-permute-done.1.rows_ref, bf16[768,512]{1,0:T(8,128)(2,1)S(1)} %fusion.9.self_ref, bf16[768,512]{1,0:T(8,128)(2,1)S(1)} %fusion.8.neigh_ref, f32[1,512]{1,0:T(1,128)S(1)} %bitcast.27, ...), custom_call_target="tpu_custom_call" | custom-call | tf_op jit(solution)/shard_map/layer_second/pallas_call | solution.py:272
  153.9 4.8 %all-to-all-start.2 = ((bf16[16,32,1664]{2,1,0:T(8,128)(2,1)}), bf16[16,32,1664]{2,1,0:T(8,128)(2,1)S(1)}, u32[]{:S(2)}, u32[]{:S(2)}) async-start(bf16[16,32,1664]{2,1,0:T(8,128)(2,1)} %bitcast.29), calls=%async_computation.2 | async-start | bytes 3407872 | tf_op jit(solution)/shard_map/all_to_all | solution.py:339
  158.7 0.0 collective-permute-start.2
  158.8 1.2 fusion
  160.0 23.4 %all-to-all-done.2.pieces_ref = bf16[16,32,1664]{2,1,0:T(8,128)(2,1)S(1)} async-done(((bf16[16,32,1664]{2,1,0:T(8,128)(2,1)}), bf16[16,32,1664]{2,1,0:T(8,128)(2,1)S(1)}, u32[]{:S(2)}, u32[]{:S(2)}) %all-to-all-start.2) | async-done | bytes 1703968 | tf_op jit(solution)/shard_map/all_to_all | solution.py:339
  183.4 0.9 sum_pieces.1
  184.3 3.4 %all-to-all-start.3 = ((bf16[8,4,1664]{2,1,0:T(4,128)(2,1)}), bf16[8,4,1664]{2,1,0:T(4,128)(2,1)S(1)}, u32[]{:S(2)}, u32[]{:S(2)}) async-start(bf16[8,4,1664]{2,1,0:T(4,128)(2,1)} %sum_pieces.1), calls=%async_computation.3 | async-start | bytes 212992 | tf_op jit(solution)/shard_map/all_to_all | solution.py:339
  187.6 0.0 collective-permute-done.2
  187.6 2.1 %fusion.11 = bf16[64,1024]{1,0:T(8,128)(2,1)} fusion(f32[64,1024]{1,0:T(8,128)} %fusion, bf16[64,512]{1,0:T(8,128)(2,1)S(1)} %collective-permute-done.2, s32[512]{0:T(512)S(1)} %bitcast.38), kind=kOutput, calls=%fused_computation.15 | convolution fusion | flops 67764224 | bytes 460800 | tf_op jit(solution)/shard_map/dot_general | solution.py:33
  189.8 6.6 %all-to-all-done.3.pieces_ref = bf16[8,4,1664]{2,1,0:T(4,128)(2,1)S(1)} async-done(((bf16[8,4,1664]{2,1,0:T(4,128)(2,1)}), bf16[8,4,1664]{2,1,0:T(4,128)(2,1)S(1)}, u32[]{:S(2)}, u32[]{:S(2)}) %all-to-all-start.3) | async-done | bytes 106528 | tf_op jit(solution)/shard_map/all_to_all | solution.py:339
  196.4 0.6 last.1
  (3 shorter events, 0.0 us)
Async XLA Ops:
  0.6 44.8 %copy-start = (bf16[768,1024]{1,0:T(8,128)(2,1)S(1)}, bf16[768,1024]{1,0:T(8,128)(2,1)}, u32[]{:S(2)}) copy-start(bf16[768,1024]{1,0:T(8,128)(2,1)} %param.13) | copy-start | bytes 4718596
  35.2 8.1 %copy-start.2 = (bf16[64,1024]{1,0:T(8,128)(2,1)S(1)}, bf16[64,1024]{1,0:T(8,128)(2,1)}, u32[]{:S(2)}) copy-start(bf16[64,1024]{1,0:T(8,128)(2,1)} %param.16) | copy-start | bytes 393220
  35.2 8.9 %copy-start.6 = (s32[64]{0:T(128)S(1)}, s32[64]{0:T(128)}, u32[]{:S(2)}) copy-start(s32[64]{0:T(128)} %param.10) | copy-start | bytes 772
  35.2 8.9 %copy-start.1 = (bf16[1024,768]{1,0:T(8,128)(2,1)S(1)}, bf16[1024,768]{1,0:T(8,128)(2,1)}, u32[]{:S(2)}) copy-start(bf16[1024,768]{1,0:T(8,128)(2,1)} %features_hbm.1) | copy-start | bytes 4718596
  35.3 9.7 %copy-start.4 = (s32[2,512]{1,0:T(2,128)S(1)}, s32[2,512]{1,0:T(2,128)}, u32[]{:S(2)}) copy-start(s32[2,512]{1,0:T(2,128)} %constant.26.clone) | copy-start | bytes 12292
  35.3 108.9 %all-to-all-start.1 = ((bf16[256,33,2,128]{3,2,1,0:T(2,128)(2,1)}), bf16[256,33,2,128]{3,2,1,0:T(2,128)(2,1)}, u32[]{:S(2)}, u32[]{:S(2)}) async-start(bf16[256,33,2,128]{3,2,1,0:T(2,128)(2,1)} %bitcast.28), calls=%async_computation.1 | async-start | bytes 8650752 | tf_op jit(solution)/shard_map/all_to_all | solution.py:339
  44.0 4.2 %collective-permute-start = (bf16[64,1024]{1,0:T(8,128)(2,1)}, bf16[64,1024]{1,0:T(8,128)(2,1)}, u32[]{:S(2)}, u32[]{:S(2)}) collective-permute-start(bf16[64,1024]{1,0:T(8,128)(2,1)} %multiply_convert_fusion), channel_id=1, source_target_pairs={{0,1},{1,0},{2,3},{3,2},{4,5},{5,4},{6,7},{7,6},{8,9},{9,8},{10,11... | collective-permute-start | bytes 393224 | tf_op jit(solution)/shard_map/ppermute | solution.py:343
  45.4 1.4 copy-start.5
  46.9 1.0 copy-start.3
  148.0 2.9 %collective-permute-start.1 = (bf16[384,1536]{1,0:T(8,128)(2,1)S(1)}, bf16[384,1536]{1,0:T(8,128)(2,1)S(1)}, u32[]{:S(2)}, u32[]{:S(2)}) collective-permute-start(bf16[384,1536]{1,0:T(8,128)(2,1)S(1)} %unpack.1.rows_ref.own_ref), channel_id=1, source_target_pairs={{0,1},{1,0},{2,3},{3,2},{4,5},{5,4},{6,7},{7,6},{8,9},{9,8},{10,11... | collective-permute-start | bytes 3538952 | tf_op jit(solution)/shard_map/ppermute | solution.py:343
  153.9 29.5 %all-to-all-start.2 = ((bf16[16,32,1664]{2,1,0:T(8,128)(2,1)}), bf16[16,32,1664]{2,1,0:T(8,128)(2,1)S(1)}, u32[]{:S(2)}, u32[]{:S(2)}) async-start(bf16[16,32,1664]{2,1,0:T(8,128)(2,1)} %bitcast.29), calls=%async_computation.2 | async-start | bytes 3407872 | tf_op jit(solution)/shard_map/all_to_all | solution.py:339
  158.7 28.9 %collective-permute-start.2 = (bf16[64,512]{1,0:T(8,128)(2,1)S(1)}, bf16[64,512]{1,0:T(8,128)(2,1)S(1)}, u32[]{:S(2)}, u32[]{:S(2)}) collective-permute-start(bf16[64,512]{1,0:T(8,128)(2,1)S(1)} %get-tuple-element.35), channel_id=1, source_target_pairs={{0,1},{1,0},{2,3},{3,2},{4,5},{5,4},{6,7},{7,6},{8,9},{9,8},{10,11... | collective-permute-start | bytes 196616 | tf_op jit(solution)/shard_map/ppermute | solution.py:343
  184.3 12.1 %all-to-all-start.3 = ((bf16[8,4,1664]{2,1,0:T(4,128)(2,1)}), bf16[8,4,1664]{2,1,0:T(4,128)(2,1)S(1)}, u32[]{:S(2)}, u32[]{:S(2)}) async-start(bf16[8,4,1664]{2,1,0:T(4,128)(2,1)} %sum_pieces.1), calls=%async_computation.3 | async-start | bytes 212992 | tf_op jit(solution)/shard_map/all_to_all | solution.py:339
